TPU v7x, 768 devices: a whole 4x8x12 slice. The times are simulated.
768 devices in a mesh: grp: 48 (over y_lo, z), blk: 16 (over y_hi, x, core).
Axes of the slice: x: 4, y: 8 (y_hi: 2, y_lo: 4; y = y_hi * 4 + y_lo), z: 12, core: 2. Of those that a mesh axis runs over, the one named last changes fastest.
Arguments:
- query: bfloat16 [98304, 512], P(('grp', 'blk')), may hold values from -6 to 6
- key: bfloat16 [98304, 512], P(('grp', 'blk')), may hold values from -6 to 6
- value: bfloat16 [98304, 512], P(('grp', 'blk')), may hold values from -6 to 6
- gate_u: bfloat16 [98304, 512], P(('grp', 'blk')), may hold values from -6 to 6
- out_grad: bfloat16 [98304, 1024], P(('grp', 'blk')), may hold values from -6 to 6
- lengths: int32 [48], P('grp'), may hold values from 32 to 2048
- norm_gain: float32 [512], replicated, may hold values from 0.1 to 1.9
- out_weight: bfloat16 [512, 1024], replicated, may hold values from -0.25 to 0.25
Outputs:
- layer_out: bfloat16 [98304, 1024], P(('grp', 'blk'))
- grad_query: bfloat16 [98304, 512], P(('grp', 'blk'))
- grad_key: bfloat16 [98304, 512], P(('grp', 'blk'))
- grad_value: bfloat16 [98304, 512], P(('grp', 'blk'))
- grad_gate: bfloat16 [98304, 512], P(('grp', 'blk'))
- grad_weight: float32 [512, 1024], P(None, 'blk')
Inputs may be any that keep to these rules, and one draw needn't show every extreme that they name: `lengths`: events of a user at or past its length are padding.
All inputs are finite; a program needn't handle non-finite values.
Results may differ from a plain program's by a relative error of at most 0.009.
Values may be sent and summed in bfloat16 or wider, within the bound.
A program may use at most 64 MiB of HBM per device.

v0:
```python
import math

import jax
import jax.numpy as jnp
from jax import lax
from jax.sharding import PartitionSpec as P

HEADS = 8
HEAD = 64


EPS = 1e-05


def in_one_piece(arrays, axis, split_dim, concat_dim, along):
    ends, at = ([], 0)
    for a in arrays[:-1]:
        at += a.shape[along]
        ends.append(at)
    both = jnp.concatenate(arrays, axis=along)
    return tuple(
        jnp.split(
            lax.all_to_all(both, axis, split_axis=split_dim, concat_axis=concat_dim, tiled=True),
            ends,
            axis=along,
        )
    )


def causal_mask(query_pos, key_pos, length):
    return (
        (key_pos[None, :] <= query_pos[:, None])
        & (query_pos[:, None] < length)
        & (key_pos[None, :] < length)
    )


def over_blocks(total_rows, step_fn, initial):
    size = math.gcd(total_rows, 512)

    def advance(index, carry):
        return step_fn(carry, index * size, size)

    return lax.fori_loop(0, total_rows // size, advance, initial)


def guarded(is_live, work, carry):
    return lax.cond(is_live, work, lambda held: held, carry)


def shards(query, key, value, gate_u, out_grad, lengths, norm_gain, out_weight):
    rows = query.shape[0]
    scale = HEAD ** (-0.5)
    length = lengths[0]
    lanes = lax.axis_size("blk")
    position = lax.axis_index("blk")
    per_head = max(1, lanes // HEADS)
    heads_dev = max(1, HEADS // lanes)
    head_groups = HEADS // heads_dev
    feats = heads_dev * HEAD
    stripe = rows // per_head
    member = position % per_head
    total_len = rows * lanes

    def rows_to_heads(array):
        parts = array.reshape(per_head, stripe, head_groups, feats).transpose(1, 2, 0, 3)
        return parts.reshape(stripe, lanes, feats)

    def heads_to_rows(array):
        parts = array.reshape(stripe, head_groups, per_head, feats).transpose(2, 0, 1, 3)
        return parts.reshape(rows, HEADS * HEAD)

    key_send = jnp.repeat(key.reshape(rows, head_groups, feats), per_head, axis=1)
    value_send = jnp.repeat(value.reshape(rows, head_groups, feats), per_head, axis=1)
    keys_mine, values_mine = in_one_piece((key_send, value_send), "blk", 1, 0, 2)
    query_mine = lax.all_to_all(
        rows_to_heads(query), "blk", split_axis=1, concat_axis=0, tiled=True
    )
    mine_pos = (
        jnp.arange(lanes, dtype=jnp.int32)[:, None] * rows
        + member * stripe
        + jnp.arange(stripe, dtype=jnp.int32)[None, :]
    ).reshape(lanes * stripe)
    mine_low = member * stripe
    mine_high = (lanes - 1) * rows + (member + 1) * stripe - 1
    mine_zero = jnp.zeros((lanes * stripe, heads_dev, HEAD), jnp.float32)

    def heads_live(begin):
        return (begin <= mine_high) & (begin < length) & (mine_low < length)

    def head_forward(carry, begin, size):

        def work(held):
            key_block = lax.dynamic_slice_in_dim(keys_mine, begin, size, 0)
            value_block = lax.dynamic_slice_in_dim(values_mine, begin, size, 0)
            scores = (
                jnp.einsum(
                    "rhd,nhd->hrn", query_mine, key_block, preferred_element_type=jnp.float32
                )
                * scale
            )
            mask = causal_mask(mine_pos, begin + jnp.arange(size, dtype=jnp.int32), length)
            weights = (jax.nn.silu(scores) * mask[None]).astype(jnp.bfloat16)
            return held + jnp.einsum(
                "hrn,nhd->rhd", weights, value_block, preferred_element_type=jnp.float32
            )

        return guarded(heads_live(begin), work, carry)

    attended_mine = over_blocks(total_len, head_forward, mine_zero)
    attended_back = lax.all_to_all(attended_mine, "blk", split_axis=0, concat_axis=1, tiled=True)
    attended = heads_to_rows(attended_back)
    centre = attended - jnp.mean(attended, axis=1, keepdims=True)
    inv_std = lax.rsqrt(jnp.mean(centre * centre, axis=1, keepdims=True) + EPS)
    normed = centre * inv_std
    scaled = normed * norm_gain
    gates = gate_u.astype(jnp.float32)
    mixed = (scaled * gates).astype(jnp.bfloat16)
    layer_out = jnp.dot(mixed, out_weight, preferred_element_type=jnp.float32).astype(jnp.bfloat16)
    mixed_grad = lax.dot_general(
        out_grad, out_weight, (((1,), (1,)), ((), ())), preferred_element_type=jnp.float32
    )
    grad_gate = (mixed_grad * scaled).astype(jnp.bfloat16)
    normed_grad = mixed_grad * gates * norm_gain
    attended_grad = inv_std * (
        normed_grad
        - jnp.mean(normed_grad, axis=1, keepdims=True)
        - normed * jnp.mean(normed_grad * normed, axis=1, keepdims=True)
    )
    attended_grad = attended_grad.astype(jnp.bfloat16)
    weight_term = lax.dot_general(
        mixed, out_grad, (((0,), (0,)), ((), ())), preferred_element_type=jnp.float32
    )
    grad_mine = lax.all_to_all(
        rows_to_heads(attended_grad), "blk", split_axis=1, concat_axis=0, tiled=True
    )
    full_zero = jnp.zeros((total_len, heads_dev, HEAD), jnp.float32)

    def head_backward(carry, begin, size):

        def work(held):
            query_acc, key_full, value_full = held
            key_block = lax.dynamic_slice_in_dim(keys_mine, begin, size, 0)
            value_block = lax.dynamic_slice_in_dim(values_mine, begin, size, 0)
            scores = (
                jnp.einsum(
                    "rhd,nhd->hrn", query_mine, key_block, preferred_element_type=jnp.float32
                )
                * scale
            )
            mask = causal_mask(mine_pos, begin + jnp.arange(size, dtype=jnp.int32), length)
            weights = (jax.nn.silu(scores) * mask[None]).astype(jnp.bfloat16)
            sigma = jax.nn.sigmoid(scores)
            prob_grad = jnp.einsum(
                "rhd,nhd->hrn", grad_mine, value_block, preferred_element_type=jnp.float32
            )
            score_grad = (prob_grad * sigma * (1.0 + scores * (1.0 - sigma)) * mask[None]).astype(
                jnp.bfloat16
            )
            query_acc = query_acc + jnp.einsum(
                "hrn,nhd->rhd", score_grad, key_block, preferred_element_type=jnp.float32
            )
            key_part = jnp.einsum(
                "hrn,rhd->nhd", score_grad, query_mine, preferred_element_type=jnp.float32
            )
            value_part = jnp.einsum(
                "hrn,rhd->nhd", weights, grad_mine, preferred_element_type=jnp.float32
            )
            key_full = lax.dynamic_update_slice_in_dim(key_full, key_part, begin, 0)
            value_full = lax.dynamic_update_slice_in_dim(value_full, value_part, begin, 0)
            return (query_acc, key_full, value_full)

        return guarded(heads_live(begin), work, carry)

    query_acc, key_full, value_full = over_blocks(
        total_len, head_backward, (mine_zero, full_zero, full_zero)
    )
    query_send = (query_acc * scale).astype(jnp.bfloat16)
    grad_query = heads_to_rows(
        lax.all_to_all(query_send, "blk", split_axis=0, concat_axis=1, tiled=True)
    )
    key_back, value_back = tuple(
        (
            part.astype(jnp.float32)
            for part in in_one_piece(
                (key_full.astype(jnp.bfloat16), value_full.astype(jnp.bfloat16)), "blk", 0, 1, 2
            )
        )
    )
    key_sum = (
        key_back.reshape(rows, head_groups, per_head, feats).sum(axis=2).reshape(rows, HEADS * HEAD)
    )
    value_sum = (
        value_back.reshape(rows, head_groups, per_head, feats)
        .sum(axis=2)
        .reshape(rows, HEADS * HEAD)
    )
    grad_key = (key_sum * scale).astype(jnp.bfloat16)
    grad_value = value_sum.astype(jnp.bfloat16)
    column_part = lax.psum_scatter(weight_term, "blk", scatter_dimension=1, tiled=True)
    grad_weight = lax.psum(column_part, "grp")
    return (layer_out, grad_query, grad_key, grad_value, grad_gate, grad_weight)


def solution(mesh):
    return jax.shard_map(
        shards,
        mesh=mesh,
        in_specs=(
            P(("grp", "blk"), None),
            P(("grp", "blk"), None),
            P(("grp", "blk"), None),
            P(("grp", "blk"), None),
            P(("grp", "blk"), None),
            P("grp"),
            P(),
            P(),
        ),
        out_specs=(
            P(("grp", "blk"), None),
            P(("grp", "blk"), None),
            P(("grp", "blk"), None),
            P(("grp", "blk"), None),
            P(("grp", "blk"), None),
            P(None, "blk"),
        ),
        check_vma=False,
    )
```

profile of v0, /device:TPU:6, one launch (start us, length us, event | category | flops | bytes accessed | tf_op | source)
XLA Modules:
  0.0 617.2 jit_solution(16538144728364699651)
XLA Ops:
  7.2 1.2 reshape.214
  8.4 0.2 copy.106
  8.6 0.9 reshape.228
  9.5 12.8 %all-to-all-start.1 = ((bf16[16,2,2048]{2,1,0:T(2,128)(2,1)}), bf16[16,2,2048]{2,1,0:T(2,128)(2,1)S(1)}, u32[]{:S(2)}, u32[]{:S(2)}) async-start(bf16[16,2,2048]{2,1,0:T(2,128)(2,1)} %reshape.228), calls=%async_computation.1 | async-start | bytes 262144 | tf_op jit(solution)/shard_map/all_to_all | solution.py:76
  22.3 1.0 copy.102
  24.1 1.1 pad_maximum_fusion.1
  25.2 5.7 all-to-all-done.1
  30.9 5.9 all-to-all-start
  37.5 0.2 reshape.229
  37.9 0.2 all_to_all.81
  38.1 12.5 %all-to-all-done = bf16[128,16,128]{2,0,1:T(8,128)(2,1)S(1)} async-done(((bf16[128,16,128]{2,0,1:T(8,128)(2,1)}), bf16[128,16,128]{2,0,1:T(8,128)(2,1)S(1)}, u32[]{:S(2)}, u32[]{:S(2)}) %all-to-all-start) | async-done | bytes 524320 | tf_op jit(solution)/shard_map/all_to_all | solution.py:23
  50.5 0.2 fusion.66
  51.2 5.6 while.39
  51.9 2.7 conditional.6
  51.9 0.7 broadcast_compare_fusion.1
  52.7 0.7 broadcast_compare_fusion
  53.4 1.2 fusion.11
  56.8 0.6 broadcast.154
  57.3 0.7 reduce.4
  58.2 0.3 reshape.230
  58.5 18.5 %all_to_all.103 = f32[16,1,4096]{2,1,0:T(1,128)S(1)} all-to-all(f32[16,1,4096]{2,1,0:T(1,128)S(1)} %reshape.230), channel_id=1, replica_groups=mesh['grp'=48,'blk'=16] {'blk'}, dimensions={0} | all-to-all | bytes 524288 | tf_op jit(solution)/shard_map/all_to_all | solution.py:111
  77.0 1.3 reduce.5
  78.3 0.7 reshape.231
  79.2 0.2 multiply_reduce_fusion
  79.4 0.3 copy.111
  80.0 0.6 fusion.65
  80.6 0.8 multiply_convert_fusion
  81.5 1.8 fusion.67
  83.6 0.2 reshape.232
  83.8 14.7 %all_to_all.102 = bf16[16,2,2048]{2,1,0:T(2,128)(2,1)S(1)} all-to-all(bf16[16,2,2048]{2,1,0:T(2,128)(2,1)S(1)} %reshape.232), channel_id=1, replica_groups=mesh['grp'=48,'blk'=16] {'blk'}, dimensions={0} | all-to-all | bytes 262144 | tf_op jit(solution)/shard_map/all_to_all | solution.py:134
  98.5 0.2 reshape.233
  99.0 8.8 %while.40 = (s32[]{:T(128)}, f32[1024,1,64]{0,2,1:T(8,128)S(1)}, bf16[2048,1,64]{0,2,1:T(8,128)(2,1)S(1)}, bf16[2048,1,64]{0,2,1:T(8,128)(2,1)S(1)}, s32[]{:T(12...) while((s32[]{:T(128)}, f32[1024,1,64]{0,2,1:T(8,128)S(1)}, ...), condition=%wide.region_11.12_spmd.clone, body=%wide.region_8.11_spmd.clone.sunk | while | flops 348196352 | bytes 10988484 | solution.py:44
  99.7 5.9 conditional.7
  99.7 0.7 broadcast_compare_fusion.3
  100.5 0.7 broadcast_compare_fusion.2
  101.2 0.5 fusion.47
  101.6 1.0 fusion.42
  102.7 2.2 fusion.38
  104.8 0.3 fusion.41
  105.2 0.4 fusion.43
  107.8 0.5 broadcast.156
  108.3 0.7 reduce.6
  109.2 0.9 reshape.234
  110.1 6.1 all-to-all-start.4
  116.2 0.7 copy.121
  116.9 0.7 copy.120
  117.7 3.7 pad_maximum_fusion
  121.4 12.6 %reduce.7 = bf16[2048,128]{1,0:T(8,128)(2,1)S(1)} reduce(bf16[2048,1,128]{2,1,0:T(2,128)(2,1)} %pad_maximum_fusion, bf16[]{:T(256)} %broadcast.156), dimensions={1}, to_apply=%pad_maximum_fusion.reduce_sub_computation | reduce | bytes 1048578 | tf_op jit(solution)/shard_map/concatenate | solution.py:20
  133.9 0.9 reshape.236
  134.9 9.7 %all-to-all-start.5 = ((bf16[16,2,8192]{2,1,0:T(2,128)(2,1)}), bf16[16,2,8192]{2,1,0:T(2,128)(2,1)S(1)}, u32[]{:S(2)}, u32[]{:S(2)}) async-start(bf16[16,2,8192]{2,1,0:T(2,128)(2,1)} %reshape.236), calls=%async_computation.5 | async-start | bytes 1048576 | tf_op jit(solution)/shard_map/all_to_all | solution.py:23
  144.6 1.0 convolution_convert_fusion
  145.6 1.2 reshape.235
  146.7 0.3 copy.117
  147.3 0.3 copy.118
  147.7 0.9 reshape.221
  148.6 14.2 %all-to-all-done.5 = bf16[16,2,8192]{2,1,0:T(2,128)(2,1)S(1)} async-done(((bf16[16,2,8192]{2,1,0:T(2,128)(2,1)}), bf16[16,2,8192]{2,1,0:T(2,128)(2,1)S(1)}, u32[]{:S(2)}, u32[]{:S(2)}) %all-to-all-start.5) | async-done | bytes 524320 | tf_op jit(solution)/shard_map/all_to_all | solution.py:23
  162.8 0.5 reshape.237
  163.4 0.2 bitcast_reduce_fusion
  163.8 0.8 copy.127
  164.7 0.2 copy.130
  164.9 35.4 %reduce-scatter.2.cloned.1.call-done = f32[512,64]{0,1:T(8,128)} async-done(((f32[512,1024]{0,1:T(8,128)}), f32[512,64]{0,1:T(8,128)}) %reduce-scatter.2.cloned.1.call-update) | async-done | bytes 131088 | tf_op jit(solution)/shard_map/reduce_scatter | solution.py:200
  200.3 0.8 copy.126
  201.1 407.6 %all-reduce.2.cloned.1.call-done = f32[512,64]{0,1:T(8,128)} async-done(((f32[512,64]{0,1:T(8,128)}), f32[512,64]{0,1:T(8,128)}) %all-reduce.2.cloned.1.call-update) | async-done | bytes 131088 | tf_op jit(solution)/shard_map/psum | solution.py:201
  608.7 1.6 copy.168
  (71 shorter events, 3.8 us)
Async XLA Ops:
  7.2 72.8 %copy-start = (bf16[512,1024]{1,0:T(8,128)(2,1)S(1)}, bf16[512,1024]{1,0:T(8,128)(2,1)}, u32[]{:S(2)}) copy-start(bf16[512,1024]{1,0:T(8,128)(2,1)} %param.23) | copy-start | bytes 3145732
  7.2 16.4 %copy-start.4 = (bf16[128,512]{1,0:T(8,128)(2,1)S(1)}, bf16[128,512]{1,0:T(8,128)(2,1)}, u32[]{:S(2)}) copy-start(bf16[128,512]{1,0:T(8,128)(2,1)} %param.18) | copy-start | bytes 393220
  9.5 21.3 %all-to-all-start.1 = ((bf16[16,2,2048]{2,1,0:T(2,128)(2,1)}), bf16[16,2,2048]{2,1,0:T(2,128)(2,1)S(1)}, u32[]{:S(2)}, u32[]{:S(2)}) async-start(bf16[16,2,2048]{2,1,0:T(2,128)(2,1)} %reshape.228), calls=%async_computation.1 | async-start | bytes 262144 | tf_op jit(solution)/shard_map/all_to_all | solution.py:76
  30.9 19.7 %all-to-all-start = ((bf16[128,16,128]{2,0,1:T(8,128)(2,1)}), bf16[128,16,128]{2,0,1:T(8,128)(2,1)S(1)}, u32[]{:S(2)}, u32[]{:S(2)}) async-start(bf16[128,16,128]{2,0,1:T(8,128)(2,1)} %pad_maximum_fusion.1), calls=%async_computation | async-start | bytes 1048576 | tf_op jit(solution)/shard_map/all_to_all | solution.py:23
  36.7 163.5 %reduce-scatter.2.cloned.1.call-start = ((), (), s32[]{:S(2)}) async-start(), calls=%async_computation.7 | async-start | bytes 2228224 | tf_op jit(solution)/shard_map/reduce_scatter | solution.py:200
  56.8 1.8 copy-start.3
  77.0 3.0 copy-start.1
  77.0 3.0 copy-start.2
  77.0 3.0 copy-start.5
  110.1 24.8 %all-to-all-start.4 = ((bf16[16,2,2048]{2,1,0:T(2,128)(2,1)}), bf16[16,2,2048]{2,1,0:T(2,128)(2,1)}, u32[]{:S(2)}, u32[]{:S(2)}) async-start(bf16[16,2,2048]{2,1,0:T(2,128)(2,1)} %reshape.234), calls=%async_computation.4 | async-start | bytes 262144 | tf_op jit(solution)/shard_map/all_to_all | solution.py:180
  134.9 28.0 %all-to-all-start.5 = ((bf16[16,2,8192]{2,1,0:T(2,128)(2,1)}), bf16[16,2,8192]{2,1,0:T(2,128)(2,1)S(1)}, u32[]{:S(2)}, u32[]{:S(2)}) async-start(bf16[16,2,8192]{2,1,0:T(2,128)(2,1)} %reshape.236), calls=%async_computation.5 | async-start | bytes 1048576 | tf_op jit(solution)/shard_map/all_to_all | solution.py:23
  144.5 464.2 %all-reduce.2.cloned.1.call-start = ((), (), s32[]{:S(2)}) async-start(), calls=%async_computation.8 | async-start | bytes 262144 | tf_op jit(solution)/shard_map/psum | solution.py:201
Sparse Core Ops, SparseCore 0:
  83.4 116.7 reduce-scatter.1
  203.5 405.2 all-reduce.1
where the time goes:
time: 617 us
  waiting for transfers between devices  475 us (77%)
  starting transfers between devices  34.5 us (6%)
  blocking collectives  33.2 us (5%)
  other arithmetic  24.3 us (4%)
  local copies, waits for them, and re-layouts  19.7 us (3%)
  between operations  15.1 us (2%)
  matrix products  9.06 us (1%)
    psum x1, waiting for transfers between devices, shards(): grad_weight = lax.psum(column_part, 'grp')  408 us
    reduce_scatter x1, waiting for transfers between devices, shards(): lax.psum_scatter(weight_term, 'blk', scatter_dimension=1, tiled=True)  35.4 us
    all_to_all x2, waiting for transfers between devices, in_one_piece(): lax.all_to_all(both, axis, split_axis=split_dim, concat_axis=concat_dim,...  26.7 us
    all_to_all x1, blocking collectives, shards(): lax.all_to_all(attended_mine, 'blk', split_axis=0, concat_axis=1, tiled=T...  18.5 us
    concatenate x3, other arithmetic, in_one_piece(): both = jnp.concatenate(arrays, axis=along)  17.3 us
    all_to_all x2, starting transfers between devices, in_one_piece(): lax.all_to_all(both, axis, split_axis=split_dim, concat_axis=concat_dim,...  15.5 us
    all_to_all x1, blocking collectives, shards(): lax.all_to_all(rows_to_heads(attended_grad), 'blk', split_axis=1, concat_...  14.7 us
    all_to_all x1, starting transfers between devices, shards(): lax.all_to_all(rows_to_heads(query), 'blk', split_axis=1, concat_axis=0,...  12.8 us
  transfers between devices with their start and end apart: 6, of which 5 were waited for; matrix products, arithmetic and copies ran while one was open for 6% of the time, Pallas kernels for 0%

commit v1 on v0

--- a/solution.py
+++ b/solution.py
@@ -3,6 +3,8 @@
 import jax
 import jax.numpy as jnp
 from jax import lax
+from jax.experimental import pallas as pl
+from jax.experimental.pallas import tpu as pltpu
 from jax.sharding import PartitionSpec as P
 
 HEADS = 8
@@ -10,6 +12,170 @@
 
 
 EPS = 1e-05
+
+
+MESH = pl.DeviceIdType.MESH
+NZ = 12
+NYL = 4
+NX = 4
+
+
+def where_am_i():
+    g, b = (lax.axis_index("grp"), lax.axis_index("blk"))
+    return (g // NZ, g % NZ, b // 8, (b // 2) % NX, b % 2)
+
+
+def device(y_lo, z, y_hi, x, core):
+    return (y_lo * NZ + z, (y_hi * NX + x) * 2 + core)
+
+
+def remote(src, dst, send_sem, recv_sem, target):
+    return pltpu.make_async_remote_copy(
+        src_ref=src, dst_ref=dst, send_sem=send_sem, recv_sem=recv_sem,
+        device_id=target, device_id_type=MESH,
+    )
+
+
+def weight_partners(me):
+    y_lo, z, y_hi, x, core = me
+    y = y_hi * NYL + y_lo
+    found = [device(y_lo, z, y_hi, x, 1 - core)]
+    for d in range(1, NX):
+        found.append(device(y_lo, z, y_hi, (x + d) % NX, core))
+    for d in range(1, 8):
+        to = (y + d) % 8
+        found.append(device(to % NYL, z, to // NYL, x, core))
+    for d in range(1, NZ):
+        found.append(device(y_lo, (z + d) % NZ, y_hi, x, core))
+    return found
+
+
+def weight_kernel(
+    mixed_ref, cot_ref, out_ref,
+    term, term_send, core_got, x_own, x_send, x_got, y_own, y_send, y_got, z_all, gathered,
+    core_sem, x_ssem, x_rsem, y_ssem, y_rsem, z_ssem, z_rsem, g_ssem, g_rsem,
+):
+    me = where_am_i()
+    y_lo, z, y_hi, x, core = me
+    y = y_hi * NYL + y_lo
+    barrier = pltpu.get_barrier_semaphore()
+    partners = weight_partners(me)
+    for target in partners:
+        pl.semaphore_signal(barrier, inc=1, device_id=target, device_id_type=MESH)
+
+    mixed = mixed_ref[...]
+    for hi in range(2):
+        for xx in range(NX):
+            block = hi * NX + xx
+            part = lax.dot_general(
+                cot_ref[:, block * 128:(block + 1) * 128], mixed,
+                (((0,), (0,)), ((), ())), preferred_element_type=jnp.float32,
+            )
+            for cc in range(2):
+                piece = part[cc * 64:(cc + 1) * 64]
+                term[cc, xx, hi] = piece
+                term_send[cc, xx, hi] = piece.astype(jnp.bfloat16)
+    pl.semaphore_wait(barrier, len(partners))
+
+    to_core = remote(
+        term_send.at[1 - core], core_got, core_sem.at[0], core_sem.at[1],
+        device(y_lo, z, y_hi, x, 1 - core),
+    )
+    to_core.start()
+    to_core.wait_recv()
+    sends = [to_core]
+    for d in range(1, NX):
+        xx = (x + d) % NX
+        x_send[d] = (term[core, xx] + core_got[xx].astype(jnp.float32)).astype(jnp.bfloat16)
+        copy = remote(
+            x_send.at[d], x_got.at[d], x_ssem.at[d], x_rsem.at[d],
+            device(y_lo, z, y_hi, xx, core),
+        )
+        copy.start()
+        sends.append(copy)
+    x_own[...] = term[core, x] + core_got[x].astype(jnp.float32)
+    for d in range(1, NX):
+        sends[d].wait_recv()
+        x_own[...] += x_got[d].astype(jnp.float32)
+    for hi in range(2):
+        for lo in range(NYL):
+            piece = x_own[hi, lo * 16:(lo + 1) * 16]
+            y_own[hi * NYL + lo] = piece
+            y_send[hi * NYL + lo] = piece.astype(jnp.bfloat16)
+    to_y = []
+    for d in range(1, 8):
+        to = (y + d) % 8
+        copy = remote(
+            y_send.at[to], y_got.at[d], y_ssem.at[d], y_rsem.at[d],
+            device(to % NYL, z, to // NYL, x, core),
+        )
+        copy.start()
+        to_y.append(copy)
+    total = y_own[y]
+    for d in range(1, 8):
+        to_y[d - 1].wait_recv()
+        total = total + y_got[d].astype(jnp.float32)
+    z_all[z] = total.astype(jnp.bfloat16)
+    to_z = []
+    for d in range(1, NZ):
+        copy = remote(
+            z_all.at[z], z_all.at[z], z_ssem.at[d], z_rsem.at[d],
+            device(y_lo, (z + d) % NZ, y_hi, x, core),
+        )
+        copy.start()
+        to_z.append(copy)
+    for d in range(1, NZ):
+        remote(
+            z_all.at[z], z_all.at[(z + NZ - d) % NZ], z_ssem.at[d], z_rsem.at[d],
+            device(y_lo, (z + d) % NZ, y_hi, x, core),
+        ).wait_recv()
+    total = z_all[0].astype(jnp.float32)
+    for zz in range(1, NZ):
+        total = total + z_all[zz].astype(jnp.float32)
+    gathered[y_lo] = total
+    to_g = []
+    for d in range(1, NYL):
+        copy = remote(
+            gathered.at[y_lo], gathered.at[y_lo], g_ssem.at[d], g_rsem.at[d],
+            device((y_lo + d) % NYL, z, y_hi, x, core),
+        )
+        copy.start()
+        to_g.append(copy)
+    for d in range(1, NYL):
+        remote(
+            gathered.at[y_lo], gathered.at[(y_lo + NYL - d) % NYL], g_ssem.at[d], g_rsem.at[d],
+            device((y_lo + d) % NYL, z, y_hi, x, core),
+        ).wait_recv()
+    out_ref[...] = gathered[...].reshape(64, 512).T
+    for copy in sends + to_y + to_z + to_g:
+        copy.wait_send()
+
+
+def weight_reduce(mixed, cotangent):
+    f32, bf16, dma = (jnp.float32, jnp.bfloat16, pltpu.SemaphoreType.DMA)
+    vmem = pltpu.VMEM
+    return pl.pallas_call(
+        weight_kernel,
+        out_shape=jax.ShapeDtypeStruct((512, 64), f32),
+        in_specs=[pl.BlockSpec(memory_space=vmem)] * 2,
+        out_specs=pl.BlockSpec(memory_space=vmem),
+        scratch_shapes=[
+            vmem((2, NX, 2, 64, 512), f32),
+            vmem((2, NX, 2, 64, 512), bf16),
+            vmem((NX, 2, 64, 512), bf16),
+            vmem((2, 64, 512), f32),
+            vmem((NX, 2, 64, 512), bf16),
+            vmem((NX, 2, 64, 512), bf16),
+            vmem((8, 16, 512), f32),
+            vmem((8, 16, 512), bf16),
+            vmem((8, 16, 512), bf16),
+            vmem((NZ, 16, 512), bf16),
+            vmem((NYL, 16, 512), f32),
+            dma((2,)), dma((NX,)), dma((NX,)), dma((8,)), dma((8,)),
+            dma((NZ,)), dma((NZ,)), dma((NYL,)), dma((NYL,)),
+        ],
+        compiler_params=pltpu.CompilerParams(collective_id=0, has_side_effects=True),
+    )(mixed, cotangent)
 
 
 def in_one_piece(arrays, axis, split_dim, concat_dim, along):
@@ -128,9 +294,6 @@
         - normed * jnp.mean(normed_grad * normed, axis=1, keepdims=True)
     )
     attended_grad = attended_grad.astype(jnp.bfloat16)
-    weight_term = lax.dot_general(
-        mixed, out_grad, (((0,), (0,)), ((), ())), preferred_element_type=jnp.float32
-    )
     grad_mine = lax.all_to_all(
         rows_to_heads(attended_grad), "blk", split_axis=1, concat_axis=0, tiled=True
     )
@@ -197,8 +360,7 @@
     )
     grad_key = (key_sum * scale).astype(jnp.bfloat16)
     grad_value = value_sum.astype(jnp.bfloat16)
-    column_part = lax.psum_scatter(weight_term, "blk", scatter_dimension=1, tiled=True)
-    grad_weight = lax.psum(column_part, "grp")
+    grad_weight = weight_reduce(mixed, out_grad)
     return (layer_out, grad_query, grad_key, grad_value, grad_gate, grad_weight)
 
 

time: 617 us -> 213 us (0.35)
  the two profiles are of different devices: /device:TPU:6 before, /device:TPU:8 now
where the time goes in v1:
time: 213 us; the launch traced here: 212 us
  Pallas kernels  54.9 us (26%)
  blocking collectives  30.5 us (14%)
  other arithmetic  29.9 us (14%)
  waiting for transfers between devices  27.1 us (13%)
  starting transfers between devices  26 us (12%)
  local copies, waits for them, and re-layouts  20.1 us (9%)
  matrix products  16 us (8%)
  loops' own time  5.96 us (3%)
    pallas_call x1, Pallas kernels, weight_reduce(): pl.pallas_call(weight_kernel, out_shape=jax.ShapeDtypeStruct((512, 64), f...  54.9 us
    all_to_all x2, waiting for transfers between devices, in_one_piece(): lax.all_to_all(both, axis, split_axis=split_dim, concat_axis=concat_dim,...  17.9 us
    concatenate x3, other arithmetic, in_one_piece(): both = jnp.concatenate(arrays, axis=along)  17.4 us
    all_to_all x1, blocking collectives, shards(): lax.all_to_all(attended_mine, 'blk', split_axis=0, concat_axis=1, tiled=T...  17.3 us
    all_to_all x1, blocking collectives, shards(): lax.all_to_all(rows_to_heads(attended_grad), 'blk', split_axis=1, concat_...  13.2 us
    all_to_all x2, starting transfers between devices, in_one_piece(): lax.all_to_all(both, axis, split_axis=split_dim, concat_axis=concat_dim,...  13.1 us
    unnamed x33, local copies, waits for them, and re-layouts  11.5 us
    all_to_all x1, waiting for transfers between devices, shards(): lax.all_to_all(rows_to_heads(query), 'blk', split_axis=1, concat_axis=0,...  9.15 us
  transfers between devices with their start and end apart: 4, of which 2 were waited for; matrix products, arithmetic and copies ran while one was open for 13% of the time, Pallas kernels for 26%

profile of v1, /device:TPU:8, one launch (start us, length us, event | category | flops | bytes accessed | tf_op | source)
XLA Modules:
  0.0 212.2 jit_solution(2508136086268557185)
XLA Ops:
  0.7 1.2 reshape.214
  2.1 0.9 reshape.228
  3.0 8.8 %all-to-all-start.1 = ((bf16[16,2,2048]{2,1,0:T(2,128)(2,1)}), bf16[16,2,2048]{2,1,0:T(2,128)(2,1)S(1)}, u32[]{:S(2)}, u32[]{:S(2)}) async-start(bf16[16,2,2048]{2,1,0:T(2,128)(2,1)} %reshape.228), calls=%async_computation.1 | async-start | bytes 262144 | tf_op jit(solution)/shard_map/all_to_all | solution.py:242
  11.8 1.0 copy.107
  13.5 1.1 pad_maximum_fusion.1
  14.6 9.1 %all-to-all-done.1 = bf16[16,2,2048]{2,1,0:T(2,128)(2,1)S(1)} async-done(((bf16[16,2,2048]{2,1,0:T(2,128)(2,1)}), bf16[16,2,2048]{2,1,0:T(2,128)(2,1)S(1)}, u32[]{:S(2)}, u32[]{:S(2)}) %all-to-all-start.1) | async-done | bytes 131104 | tf_op jit(solution)/shard_map/all_to_all | solution.py:242
  23.8 3.6 %all-to-all-start = ((bf16[128,16,128]{2,0,1:T(8,128)(2,1)}), bf16[128,16,128]{2,0,1:T(8,128)(2,1)S(1)}, u32[]{:S(2)}, u32[]{:S(2)}) async-start(bf16[128,16,128]{2,0,1:T(8,128)(2,1)} %pad_maximum_fusion.1), calls=%async_computation | async-start | bytes 1048576 | tf_op jit(solution)/shard_map/all_to_all | solution.py:189
  28.6 17.9 %all-to-all-done = bf16[128,16,128]{2,0,1:T(8,128)(2,1)S(1)} async-done(((bf16[128,16,128]{2,0,1:T(8,128)(2,1)}), bf16[128,16,128]{2,0,1:T(8,128)(2,1)S(1)}, u32[]{:S(2)}, u32[]{:S(2)}) %all-to-all-start) | async-done | bytes 524320 | tf_op jit(solution)/shard_map/all_to_all | solution.py:189
  47.2 11.0 %while.39 = (s32[]{:T(128)}, f32[1024,1,64]{0,2,1:T(8,128)S(1)}, s32[]{:T(128)}, s32[]{:T(128)}, pred[]{:T(512)}, /*index=5*/bf16[2048,1,64]{0,2,1:T(8,128)(2,1)...) while((s32[]{:T(128)}, f32[1024,1,64]{0,2,1:T(8,128)S(1)}, ...), condition=%wide.region_3.4_spmd.clone, body=%wide.region_0.3_spmd.clone.sunk | while | flops 139529728 | bytes 823632 | solution.py:210
  47.9 2.7 %conditional.6 = (f32[1024,1,64]{0,2,1:T(8,128)S(1)}) conditional(s32[]{:T(128)} %convert_element_type.115, f32[1024,1,64]{0,2,1:T(8,128)S(1)} %get-tuple-element.985, (s32[]{:T(128)}, bf16[2048,1,64]{0,2,1:T(8,128)(2,1)S(1)}, s32[16]{0:T(128)S(1)}, s32[]{:T(128)}, bf16[2048,1,64]{0,2,1:T(8,128)(2,1)S(1)}, ...), branch_computations={%region_1.1_spmd, %region_2.2_spmd} | conditional | flops 139529728 | bytes 819322 | solution.py:214
  47.9 0.7 broadcast_compare_fusion.1
  48.8 0.7 broadcast_compare_fusion
  49.4 1.2 fusion.11
  51.3 2.7 %conditional.6 = (f32[1024,1,64]{0,2,1:T(8,128)S(1)}) conditional(s32[]{:T(128)} %convert_element_type.115, f32[1024,1,64]{0,2,1:T(8,128)S(1)} %get-tuple-element.985, (s32[]{:T(128)}, bf16[2048,1,64]{0,2,1:T(8,128)(2,1)S(1)}, s32[16]{0:T(128)S(1)}, s32[]{:T(128)}, bf16[2048,1,64]{0,2,1:T(8,128)(2,1)S(1)}, ...), branch_computations={%region_1.1_spmd, %region_2.2_spmd} | conditional | flops 139529728 | bytes 819322 | solution.py:214
  51.4 0.7 broadcast_compare_fusion.1
  52.2 0.7 broadcast_compare_fusion
  52.8 1.2 fusion.11
  54.8 2.7 %conditional.6 = (f32[1024,1,64]{0,2,1:T(8,128)S(1)}) conditional(s32[]{:T(128)} %convert_element_type.115, f32[1024,1,64]{0,2,1:T(8,128)S(1)} %get-tuple-element.985, (s32[]{:T(128)}, bf16[2048,1,64]{0,2,1:T(8,128)(2,1)S(1)}, s32[16]{0:T(128)S(1)}, s32[]{:T(128)}, bf16[2048,1,64]{0,2,1:T(8,128)(2,1)S(1)}, ...), branch_computations={%region_1.1_spmd, %region_2.2_spmd} | conditional | flops 139529728 | bytes 819322 | solution.py:214
  54.8 0.7 broadcast_compare_fusion.1
  55.6 0.7 broadcast_compare_fusion
  56.3 1.2 fusion.11
  58.2 0.5 broadcast.154
  58.7 0.7 reduce.4
  59.9 17.3 %all_to_all.103 = f32[16,1,4096]{2,1,0:T(1,128)S(1)} all-to-all(f32[16,1,4096]{2,1,0:T(1,128)S(1)} %reshape.230), channel_id=1, replica_groups=mesh['grp'=48,'blk'=16] {'blk'}, dimensions={0} | all-to-all | bytes 524288 | tf_op jit(solution)/shard_map/all_to_all | solution.py:277
  77.3 1.3 reduce.5
  78.6 0.7 reshape.231
  80.3 0.6 fusion.65
  80.9 0.9 multiply_convert_fusion
  82.3 13.2 %all_to_all.102 = bf16[16,2,2048]{2,1,0:T(2,128)(2,1)S(1)} all-to-all(bf16[16,2,2048]{2,1,0:T(2,128)(2,1)S(1)} %reshape.232), channel_id=1, replica_groups=mesh['grp'=48,'blk'=16] {'blk'}, dimensions={0} | all-to-all | bytes 262144 | tf_op jit(solution)/shard_map/all_to_all | solution.py:297
  95.9 18.1 %while.40 = (s32[]{:T(128)}, f32[1024,1,64]{0,2,1:T(8,128)S(1)}, bf16[2048,1,64]{0,2,1:T(8,128)(2,1)S(1)}, bf16[2048,1,64]{0,2,1:T(8,128)(2,1)S(1)}, s32[]{:T(12...) while((s32[]{:T(128)}, f32[1024,1,64]{0,2,1:T(8,128)S(1)}, ...), condition=%wide.region_11.12_spmd.clone, body=%wide.region_8.11_spmd.clone.sunk | while | flops 348196352 | bytes 10988484 | solution.py:210
  96.6 5.1 %conditional.7 = ((f32[1024,1,64]{0,2,1:T(8,128)S(1)}, bf16[2048,1,64]{0,2,1:T(8,128)(2,1)S(1)}, bf16[2048,1,64]{0,2,1:T(8,128)(2,1)S(1)})) conditional(s32[]{:T(128)} %convert_element_type.116, (f32[1024,1,64]{0,2,1:T(8,128)S(1)}, bf16[2048,1,64]{0,2,1:T(8,128)(2,1)S(1)}, bf16[2048,1,64]{0,2,1:T(8,128)(2,1)S(1)}) %tuple.123, (s32[]{:T(128)}, ...), branch_computations={%region_9.9_spmd, %region_10.10_spmd} | conditional | flops 348196352 | bytes 10984102 | solution.py:214
  96.6 0.7 broadcast_compare_fusion.3
  97.4 0.7 broadcast_compare_fusion.2
  98.5 1.0 fusion.42
  99.6 1.3 fusion.38
  102.4 5.1 %conditional.7 = ((f32[1024,1,64]{0,2,1:T(8,128)S(1)}, bf16[2048,1,64]{0,2,1:T(8,128)(2,1)S(1)}, bf16[2048,1,64]{0,2,1:T(8,128)(2,1)S(1)})) conditional(s32[]{:T(128)} %convert_element_type.116, (f32[1024,1,64]{0,2,1:T(8,128)S(1)}, bf16[2048,1,64]{0,2,1:T(8,128)(2,1)S(1)}, bf16[2048,1,64]{0,2,1:T(8,128)(2,1)S(1)}) %tuple.123, (s32[]{:T(128)}, ...), branch_computations={%region_9.9_spmd, %region_10.10_spmd} | conditional | flops 348196352 | bytes 10984102 | solution.py:214
  102.4 0.7 broadcast_compare_fusion.3
  103.2 0.7 broadcast_compare_fusion.2
  103.9 0.5 fusion.47
  104.3 1.0 fusion.42
  105.4 1.3 fusion.38
  108.2 5.1 %conditional.7 = ((f32[1024,1,64]{0,2,1:T(8,128)S(1)}, bf16[2048,1,64]{0,2,1:T(8,128)(2,1)S(1)}, bf16[2048,1,64]{0,2,1:T(8,128)(2,1)S(1)})) conditional(s32[]{:T(128)} %convert_element_type.116, (f32[1024,1,64]{0,2,1:T(8,128)S(1)}, bf16[2048,1,64]{0,2,1:T(8,128)(2,1)S(1)}, bf16[2048,1,64]{0,2,1:T(8,128)(2,1)S(1)}) %tuple.123, (s32[]{:T(128)}, ...), branch_computations={%region_9.9_spmd, %region_10.10_spmd} | conditional | flops 348196352 | bytes 10984102 | solution.py:214
  108.2 0.7 broadcast_compare_fusion.3
  109.0 0.7 broadcast_compare_fusion.2
  110.1 1.0 fusion.42
  111.2 1.3 fusion.38
  114.0 0.5 broadcast.156
  114.5 0.7 reduce.6
  115.4 0.9 reshape.234
  116.3 4.2 %all-to-all-start.4 = ((bf16[16,2,2048]{2,1,0:T(2,128)(2,1)}), bf16[16,2,2048]{2,1,0:T(2,128)(2,1)}, u32[]{:S(2)}, u32[]{:S(2)}) async-start(bf16[16,2,2048]{2,1,0:T(2,128)(2,1)} %reshape.234), calls=%async_computation.4 | async-start | bytes 262144 | tf_op jit(solution)/shard_map/all_to_all | solution.py:343
  120.5 0.7 copy.126
  121.2 0.7 copy.125
  122.0 3.7 %pad_maximum_fusion = bf16[2048,1,128]{2,1,0:T(2,128)(2,1)} fusion(bf16[2048,1,64]{2,1,0:T(2,128)(2,1)S(1)} %copy.126, bf16[2048,1,64]{2,1,0:T(2,128)(2,1)S(1)} %copy.125), kind=kLoop, calls=%fused_computation.75 | loop fusion | flops 1048576 | bytes 1048576 | tf_op jit(solution)/shard_map/concatenate | solution.py:186
  125.7 12.6 %reduce.7 = bf16[2048,128]{1,0:T(8,128)(2,1)S(1)} reduce(bf16[2048,1,128]{2,1,0:T(2,128)(2,1)} %pad_maximum_fusion, bf16[]{:T(256)} %broadcast.156), dimensions={1}, to_apply=%pad_maximum_fusion.reduce_sub_computation | reduce | bytes 1048578 | tf_op jit(solution)/shard_map/concatenate | solution.py:186
  138.3 0.9 reshape.236
  139.2 9.5 %all-to-all-start.5 = ((bf16[16,2,8192]{2,1,0:T(2,128)(2,1)}), bf16[16,2,8192]{2,1,0:T(2,128)(2,1)S(1)}, u32[]{:S(2)}, u32[]{:S(2)}) async-start(bf16[16,2,8192]{2,1,0:T(2,128)(2,1)} %reshape.236), calls=%async_computation.5 | async-start | bytes 1048576 | tf_op jit(solution)/shard_map/all_to_all | solution.py:189
  148.7 54.9 %shard_map.127 = f32[512,64]{1,0:T(8,128)} custom-call(bf16[128,512]{1,0:T(8,128)(2,1)} %get-tuple-element.829.mixed_ref, bf16[128,1024]{1,0:T(8,128)(2,1)} %cot_ref.1), custom_call_target="tpu_custom_call" | custom-call | tf_op jit(solution)/shard_map/pallas_call | solution.py:157
  203.6 1.7 copy.133
  205.3 1.0 convolution_convert_fusion
  206.3 1.2 reshape.235
  208.5 0.9 reshape.221
  209.4 0.5 reshape.237
  210.4 0.8 copy.132
  211.5 0.8 copy.131
  (97 shorter events, 10.6 us)
Async XLA Ops:
  0.6 79.7 %copy-start = (bf16[512,1024]{1,0:T(8,128)(2,1)S(1)}, bf16[512,1024]{1,0:T(8,128)(2,1)}, u32[]{:S(2)}) copy-start(bf16[512,1024]{1,0:T(8,128)(2,1)} %param.23) | copy-start | bytes 3145732
  0.6 12.4 %copy-start.4 = (bf16[128,512]{1,0:T(8,128)(2,1)S(1)}, bf16[128,512]{1,0:T(8,128)(2,1)}, u32[]{:S(2)}) copy-start(bf16[128,512]{1,0:T(8,128)(2,1)} %param.18) | copy-start | bytes 393220
  3.0 20.8 %all-to-all-start.1 = ((bf16[16,2,2048]{2,1,0:T(2,128)(2,1)}), bf16[16,2,2048]{2,1,0:T(2,128)(2,1)S(1)}, u32[]{:S(2)}, u32[]{:S(2)}) async-start(bf16[16,2,2048]{2,1,0:T(2,128)(2,1)} %reshape.228), calls=%async_computation.1 | async-start | bytes 262144 | tf_op jit(solution)/shard_map/all_to_all | solution.py:242
  23.8 22.8 %all-to-all-start = ((bf16[128,16,128]{2,0,1:T(8,128)(2,1)}), bf16[128,16,128]{2,0,1:T(8,128)(2,1)S(1)}, u32[]{:S(2)}, u32[]{:S(2)}) async-start(bf16[128,16,128]{2,0,1:T(8,128)(2,1)} %pad_maximum_fusion.1), calls=%async_computation | async-start | bytes 1048576 | tf_op jit(solution)/shard_map/all_to_all | solution.py:189
  77.3 3.0 %copy-start.2 = (bf16[128,1024]{1,0:T(8,128)(2,1)S(1)}, bf16[128,1024]{1,0:T(8,128)(2,1)}, u32[]{:S(2)}) copy-start(bf16[128,1024]{1,0:T(8,128)(2,1)} %cot_ref.1) | copy-start | bytes 786436
  77.3 3.0 %copy-start.3 = (bf16[128,512]{1,0:T(8,128)(2,1)S(1)}, bf16[128,512]{1,0:T(8,128)(2,1)}, u32[]{:S(2)}) copy-start(bf16[128,512]{1,0:T(8,128)(2,1)} %param.19) | copy-start | bytes 393220
  77.3 3.0 %copy-start.5 = (f32[512]{0:T(512)S(1)}, f32[512]{0:T(512)}, u32[]{:S(2)}) copy-start(f32[512]{0:T(512)} %param.22) | copy-start | bytes 6148
  116.3 22.9 %all-to-all-start.4 = ((bf16[16,2,2048]{2,1,0:T(2,128)(2,1)}), bf16[16,2,2048]{2,1,0:T(2,128)(2,1)}, u32[]{:S(2)}, u32[]{:S(2)}) async-start(bf16[16,2,2048]{2,1,0:T(2,128)(2,1)} %reshape.234), calls=%async_computation.4 | async-start | bytes 262144 | tf_op jit(solution)/shard_map/all_to_all | solution.py:343
  125.7 79.7 %copy-start.1 = (bf16[128,512]{1,0:T(8,128)(2,1)S(1)}, bf16[128,512]{1,0:T(8,128)(2,1)}, u32[]{:S(2)}) copy-start(bf16[128,512]{1,0:T(8,128)(2,1)} %get-tuple-element.829.mixed_ref) | copy-start | bytes 393220
  139.2 70.2 %all-to-all-start.5 = ((bf16[16,2,8192]{2,1,0:T(2,128)(2,1)}), bf16[16,2,8192]{2,1,0:T(2,128)(2,1)S(1)}, u32[]{:S(2)}, u32[]{:S(2)}) async-start(bf16[16,2,8192]{2,1,0:T(2,128)(2,1)} %reshape.236), calls=%async_computation.5 | async-start | bytes 1048576 | tf_op jit(solution)/shard_map/all_to_all | solution.py:189

commit v2 on v1

v2 whole, which is shorter than its diff:
```python
import jax
import jax.numpy as jnp
from jax import lax
from jax.experimental import pallas as pl
from jax.experimental.pallas import tpu as pltpu
from jax.sharding import PartitionSpec as P

MESH = pl.DeviceIdType.MESH
EPS = 1e-05
NZ = 12
NYL = 4
NX = 4
HALF = 8
ROWS = 128
TILE = 512
PIECE = 64 // NYL
F32 = jnp.float32
BF16 = jnp.bfloat16


def where_am_i():
    g, b = (lax.axis_index("grp"), lax.axis_index("blk"))
    return (g // NZ, g % NZ, b // 8, (b // 2) % NX, b % 2)


def device(y_lo, z, y_hi, x, core):
    return (y_lo * NZ + z, (y_hi * NX + x) * 2 + core)


def remote(src, dst, send_sem, recv_sem, target):
    return pltpu.make_async_remote_copy(
        src_ref=src, dst_ref=dst, send_sem=send_sem, recv_sem=recv_sem,
        device_id=target, device_id_type=MESH,
    )


def all_partners(me):
    y_lo, z, y_hi, x, core = me
    g = y_lo * NZ + z
    mine = (y_hi * NX + x) * 2 + core
    y = y_hi * NYL + y_lo
    found = [(g, (mine + d) % 16) for d in range(1, 16)]
    for d in range(1, 2 * NYL):
        if d != NYL:
            to = (y + d) % (2 * NYL)
            found.append(device(to % NYL, z, to // NYL, x, core))
    for d in range(1, NZ):
        found.append(device(y_lo, (z + d) % NZ, y_hi, x, core))
    return found


def swap(part):
    return pltpu.roll(part.astype(F32), 64, 1)


def low_lanes(rows):
    return lax.broadcasted_iota(jnp.int32, (rows, 128), 1) < 64


def fold_rows(block, odd):
    low = low_lanes(64)
    top, bottom = (block[:64], block[64:])
    if odd:
        return jnp.where(low, swap(top), bottom.astype(F32))
    return jnp.where(low, top.astype(F32), swap(bottom))


def join_heads(even, odd):
    low = low_lanes(even.shape[0])
    return (jnp.where(low, even, swap(odd)), jnp.where(low, swap(even), odd))


def nt(left, right):
    return lax.dot_general(left, right, (((1,), (1,)), ((), ())), preferred_element_type=F32)


def tn(left, right):
    return lax.dot_general(left, right, (((0,), (0,)), ((), ())), preferred_element_type=F32)


def nn(left, right):
    return jnp.dot(left, right, preferred_element_type=F32)


def layer_kernel(
    q_ref, k_ref, v_ref, gate_ref, cot_ref, length_ref, gain_ref, weight_ref,
    out_ref, gq_ref, gk_ref, gv_ref, gg_ref, gw_ref,
    in_send, in_got, up_got, qf, dof, att_acc, att_send, att_got, do_send, do_got,
    dkv_acc, dqt_acc, up_acc, back_send, back_got, down_send, down_got, mixed_grad, scaled_buf,
    mixed_buf,
    term, term_send, core_got, x_own, x_send, x_got, y_own, y_send, y_got, z_all, gathered,
    in_ss, in_rs, up_ss, up_rs, att_ss, att_rs, do_ss, do_rs, back_ss, back_rs, down_ss, down_rs,
    core_sem, x_ssem, x_rsem, y_ssem, y_rsem, z_ssem, z_rsem, g_ssem, g_rsem,
):
    me = where_am_i()
    y_lo, z, y_hi, x, core = me
    g = y_lo * NZ + z
    y = y_hi * NYL + y_lo
    h = x * 2 + core
    base = y_hi * HALF
    upper = y_hi == 1
    lower = y_hi == 0

    barrier = pltpu.get_barrier_semaphore()
    partners = all_partners(me)
    for target in partners:
        pl.semaphore_signal(barrier, inc=1, device_id=target, device_id_type=MESH)

    low128 = low_lanes(128)
    for t in range(HALF):
        cols = slice((t // 2) * 128, (t // 2 + 1) * 128)
        kk, vv = (k_ref[:, cols], v_ref[:, cols])
        if t % 2:
            pair = jnp.where(low128, swap(kk), vv.astype(F32))
        else:
            pair = jnp.where(low128, kk.astype(F32), swap(vv))
        in_send[t, 64:192] = pair.astype(BF16)
        in_send[t, 0:64] = (fold_rows(q_ref[:, cols], t % 2) * 0.0625).astype(BF16)
    in_got[h] = in_send[h]
    pl.semaphore_wait(barrier, len(partners))

    def up_copy(t):
        return remote(
            in_send.at[t, pl.ds(64, 128)], up_got.at[h], up_ss.at[t], up_rs.at[h], (g, HALF + t)
        )

    def up_arrival(s):
        return remote(
            in_send.at[s, pl.ds(64, 128)], up_got.at[s], up_ss.at[s], up_rs.at[s], (g, s)
        )

    @pl.when(lower)
    def _():
        for t in range(HALF):
            up_copy(t).start()

    def to_half(send, got, ssem, rsem):
        copies = []
        for d in range(1, HALF):
            t = (h + d) % HALF
            copies.append(remote(send.at[t], got.at[h], ssem.at[d], rsem.at[d], (g, base + t)))
        return copies

    def from_half(send, got, ssem, rsem):
        for d in range(1, HALF):
            t = (h + d) % HALF
            s = (h + HALF - d) % HALF
            remote(send.at[t], got.at[s], ssem.at[d], rsem.at[d], (g, base + t)).wait_recv()

    to_in = to_half(in_send, in_got, in_ss, in_rs)
    for copy in to_in:
        copy.start()
    mixed_grad[...] = nt(cot_ref[...], weight_ref[...])
    from_half(in_send, in_got, in_ss, in_rs)

    low64 = low_lanes(64)
    for s in range(HALF):
        folded = in_got[s, 0:64].astype(F32)
        qf[s * 128:s * 128 + 64] = jnp.where(low64, folded, 0.0).astype(BF16)
        qf[s * 128 + 64:s * 128 + 128] = jnp.where(low64, swap(folded), 0.0).astype(BF16)
    att_acc[...] = jnp.zeros_like(att_acc)

    def local_kv(j):
        return in_got[pl.ds(j * 4, 4), 64:192].reshape(TILE, 128)

    def upper_kv(j):
        return up_got[pl.ds(j * 4, 4)].reshape(TILE, 128)

    def rows_of(i):
        return pl.ds(pl.multiple_of(i * TILE, TILE), TILE)

    tile_row = lax.broadcasted_iota(jnp.int32, (TILE, TILE), 0)
    tile_col = lax.broadcasted_iota(jnp.int32, (TILE, TILE), 1)

    def forward_tile(i, kv, diagonal):
        half_score = nt(qf[rows_of(i)], kv)
        weight = half_score + half_score * jnp.tanh(half_score)
        if diagonal:
            weight = jnp.where(tile_col <= tile_row, weight, 0.0)
        att_acc[rows_of(i)] += nn(weight.astype(BF16), kv)

    @pl.loop(0, 2)
    def _(i):
        forward_tile(i, local_kv(i), True)

    forward_tile(1, local_kv(0), False)

    @pl.when(upper)
    def _():
        for s in range(HALF):
            up_arrival(s).wait_recv()

        @pl.loop(0, 4)
        def _(n):
            forward_tile(n % 2, upper_kv(n // 2), False)

    for s in range(HALF):
        top = att_acc[s * 128:s * 128 + 64]
        bottom = att_acc[s * 128 + 64:s * 128 + 128]
        att_send[s] = jnp.where(low64, swap(top), bottom).astype(BF16)
    att_got[h] = att_send[h]
    to_att = to_half(att_send, att_got, att_ss, att_rs)
    for copy in to_att:
        copy.start()
    from_half(att_send, att_got, att_ss, att_rs)

    blocks = []
    for p in range(HALF // 2):
        even, odd = (att_got[2 * p].astype(F32), att_got[2 * p + 1].astype(F32))
        top, bottom = join_heads(even, odd)
        blocks.append(jnp.concatenate([top, bottom], axis=0))
    attended = jnp.concatenate(blocks, axis=1)
    row = (base + h) * ROWS + lax.broadcasted_iota(jnp.int32, (ROWS, 512), 0)
    alive = row < length_ref[0]
    attended = jnp.where(alive, attended, 0.0)
    centre = attended - jnp.mean(attended, axis=1, keepdims=True)
    inv_std = lax.rsqrt(jnp.mean(centre * centre, axis=1, keepdims=True) + EPS)
    normed = centre * inv_std
    gain = gain_ref[...]
    scaled = normed * gain
    gates = gate_ref[...].astype(F32)
    scaled_buf[...] = scaled
    mixed_buf[...] = (scaled * gates).astype(BF16)
    normed_grad = mixed_grad[...] * gates * gain
    attended_grad = inv_std * (
        normed_grad
        - jnp.mean(normed_grad, axis=1, keepdims=True)
        - normed * jnp.mean(normed_grad * normed, axis=1, keepdims=True)
    )
    attended_grad = jnp.where(alive, attended_grad, 0.0).astype(BF16).astype(F32)
    for t in range(HALF):
        cols = slice((t // 2) * 128, (t // 2 + 1) * 128)
        do_send[t] = fold_rows(attended_grad[:, cols], t % 2).astype(BF16)
    do_got[h] = do_send[h]
    to_do = to_half(do_send, do_got, do_ss, do_rs)
    for copy in to_do:
        copy.start()

    mixed = mixed_buf[...]
    for hi in range(2):
        for xx in range(NX):
            block = hi * NX + xx
            part = tn(cot_ref[:, block * 128:(block + 1) * 128], mixed)
            for cc in range(2):
                piece = part[cc * 64:(cc + 1) * 64]
                term[cc, xx, hi] = piece
                term_send[cc, xx, hi] = piece.astype(BF16)
    to_core = remote(
        term_send.at[1 - core], core_got, core_sem.at[0], core_sem.at[1],
        device(y_lo, z, y_hi, x, 1 - core),
    )
    to_core.start()
    out_ref[...] = nn(mixed, weight_ref[...]).astype(BF16)
    gg_ref[...] = (mixed_grad[...] * scaled_buf[...]).astype(BF16)

    from_half(do_send, do_got, do_ss, do_rs)
    for s in range(HALF):
        folded = do_got[s].astype(F32)
        dof[s * 128:s * 128 + 64] = jnp.where(low64, 0.0, swap(folded)).astype(BF16)
        dof[s * 128 + 64:s * 128 + 128] = jnp.where(low64, 0.0, folded).astype(BF16)
    dkv_acc[...] = jnp.zeros_like(dkv_acc)
    dqt_acc[...] = jnp.zeros_like(dqt_acc)

    def backward_tile(i, kv, diagonal):
        qs, ds = (qf[rows_of(i)], dof[rows_of(i)])
        half_score = nt(kv, qs)
        grad = nt(kv, ds)
        tanh = jnp.tanh(half_score)
        plus = 1.0 + tanh
        weight = half_score * plus
        slope = grad * (plus + weight * (1.0 - tanh))
        if diagonal:
            keep = tile_row <= tile_col
            weight = jnp.where(keep, weight, 0.0)
            slope = jnp.where(keep, slope, 0.0)
        slope = slope.astype(BF16)
        dqt_acc[i] += tn(kv[:, :64], slope)
        return nn(slope, qs) + nn(weight.astype(BF16), ds)

    to_core.wait_recv()
    to_x = []
    for d in range(1, NX):
        xx = (x + d) % NX
        x_send[d] = (term[core, xx] + core_got[xx].astype(F32)).astype(BF16)
        copy = remote(
            x_send.at[d], x_got.at[d], x_ssem.at[d], x_rsem.at[d],
            device(y_lo, z, y_hi, xx, core),
        )
        copy.start()
        to_x.append(copy)
    x_own[...] = term[core, x] + core_got[x].astype(F32)

    def down_copy(s):
        return remote(down_send.at[s], down_got.at[h], down_ss.at[s], down_rs.at[h], (g, s))

    def down_arrival(t):
        return remote(
            down_send.at[t], down_got.at[t], down_ss.at[t], down_rs.at[t], (g, HALF + t)
        )

    @pl.when(upper)
    def _():
        up_acc[...] = jnp.zeros_like(up_acc)

        @pl.loop(0, 4)
        def _(n):
            j = n // 2
            up_acc[rows_of(j)] += backward_tile(n % 2, upper_kv(j), False)

        for s in range(HALF):
            down_send[s] = up_acc[s * 128:(s + 1) * 128].astype(BF16)
            down_copy(s).start()

    for d in range(1, NX):
        to_x[d - 1].wait_recv()
        x_own[...] += x_got[d].astype(F32)
    for hi in range(2):
        for lo in range(NYL):
            piece = x_own[hi, lo * PIECE:(lo + 1) * PIECE]
            y_own[hi * NYL + lo] = piece
            y_send[hi * NYL + lo] = piece.astype(BF16)
    to_y = []
    for d in range(1, 2 * NYL):
        to = (y + d) % (2 * NYL)
        copy = remote(
            y_send.at[to], y_got.at[d], y_ssem.at[d], y_rsem.at[d],
            device(to % NYL, z, to // NYL, x, core),
        )
        copy.start()
        to_y.append(copy)

    @pl.loop(0, 2)
    def _(i):
        dkv_acc[rows_of(i)] += backward_tile(i, local_kv(i), True)

    dkv_acc[0:TILE] += backward_tile(1, local_kv(0), False)

    for s in range(HALF):
        i, at = (s // 4, (s % 4) * 128)
        back_send[s, 0:64] = (dqt_acc[i, :, at:at + 128] * 0.0625).astype(BF16)
        back_send[s, 64:192] = dkv_acc[s * 128:(s + 1) * 128].astype(BF16)
    back_got[h] = back_send[h]
    to_back = to_half(back_send, back_got, back_ss, back_rs)
    for copy in to_back:
        copy.start()

    total = y_own[y]
    for d in range(1, 2 * NYL):
        to_y[d - 1].wait_recv()
        total = total + y_got[d].astype(F32)
    z_all[z] = total.astype(BF16)
    to_z = []
    for d in range(1, NZ):
        copy = remote(
            z_all.at[z], z_all.at[z], z_ssem.at[d], z_rsem.at[d],
            device(y_lo, (z + d) % NZ, y_hi, x, core),
        )
        copy.start()
        to_z.append(copy)

    from_half(back_send, back_got, back_ss, back_rs)
    for p in range(HALF // 2):
        cols = slice(p * 128, (p + 1) * 128)
        pair = jnp.concatenate(
            [back_got[2 * p, 0:64].astype(F32), back_got[2 * p + 1, 0:64].astype(F32)], axis=0
        )
        gq_ref[:, cols] = pair.T.astype(BF16)

    for d in range(1, NZ):
        remote(
            z_all.at[z], z_all.at[(z + NZ - d) % NZ], z_ssem.at[d], z_rsem.at[d],
            device(y_lo, (z + d) % NZ, y_hi, x, core),
        ).wait_recv()
    total = z_all[0].astype(F32)
    for zz in range(1, NZ):
        total = total + z_all[zz].astype(F32)
    gathered[y_lo] = total
    to_g = []
    for d in range(1, NYL):
        copy = remote(
            gathered.at[y_lo], gathered.at[y_lo], g_ssem.at[d], g_rsem.at[d],
            device((y_lo + d) % NYL, z, y_hi, x, core),
        )
        copy.start()
        to_g.append(copy)

    @pl.when(lower)
    def _():
        for t in range(HALF):
            down_arrival(t).wait_recv()

    for p in range(HALF // 2):
        cols = slice(p * 128, (p + 1) * 128)
        heads = []
        for t in (2 * p, 2 * p + 1):
            mine = back_got[t, 64:192].astype(F32)
            far = jnp.where(lower, down_got[t].astype(F32), 0.0)
            heads.append(mine + far)
        kk, vv = join_heads(*heads)
        gk_ref[:, cols] = kk.astype(BF16)
        gv_ref[:, cols] = vv.astype(BF16)

    for d in range(1, NYL):
        remote(
            gathered.at[y_lo], gathered.at[(y_lo + NYL - d) % NYL], g_ssem.at[d], g_rsem.at[d],
            device((y_lo + d) % NYL, z, y_hi, x, core),
        ).wait_recv()
    gw_ref[...] = gathered[...].reshape(64, 512).T

    for copy in to_in + to_att + to_do + to_back + [to_core] + to_x + to_y + to_z + to_g:
        copy.wait_send()

    @pl.when(lower)
    def _():
        for t in range(HALF):
            up_copy(t).wait_send()

    @pl.when(upper)
    def _():
        for s in range(HALF):
            down_copy(s).wait_send()


def shards(query, key, value, gate_u, out_grad, lengths, norm_gain, out_weight):
    dma = pltpu.SemaphoreType.DMA
    vmem = pltpu.VMEM
    whole = pl.BlockSpec(memory_space=vmem)
    rows = query.shape[0]
    return pl.pallas_call(
        layer_kernel,
        out_shape=(
            jax.ShapeDtypeStruct((rows, 1024), BF16),
            jax.ShapeDtypeStruct((rows, 512), BF16),
            jax.ShapeDtypeStruct((rows, 512), BF16),
            jax.ShapeDtypeStruct((rows, 512), BF16),
            jax.ShapeDtypeStruct((rows, 512), BF16),
            jax.ShapeDtypeStruct((512, 64), F32),
        ),
        in_specs=[whole] * 5 + [pl.BlockSpec(memory_space=pltpu.SMEM)] + [whole] * 2,
        out_specs=(whole,) * 6,
        scratch_shapes=[
            vmem((HALF, 192, 128), BF16),
            vmem((HALF, 192, 128), BF16),
            vmem((HALF, 128, 128), BF16),
            vmem((1024, 128), BF16),
            vmem((1024, 128), BF16),
            vmem((1024, 128), F32),
            vmem((HALF, 64, 128), BF16),
            vmem((HALF, 64, 128), BF16),
            vmem((HALF, 64, 128), BF16),
            vmem((HALF, 64, 128), BF16),
            vmem((1024, 128), F32),
            vmem((2, 64, TILE), F32),
            vmem((1024, 128), F32),
            vmem((HALF, 192, 128), BF16),
            vmem((HALF, 192, 128), BF16),
            vmem((HALF, 128, 128), BF16),
            vmem((HALF, 128, 128), BF16),
            vmem((ROWS, 512), F32),
            vmem((ROWS, 512), F32),
            vmem((ROWS, 512), BF16),
            vmem((2, NX, 2, 64, 512), F32),
            vmem((2, NX, 2, 64, 512), BF16),
            vmem((NX, 2, 64, 512), BF16),
            vmem((2, 64, 512), F32),
            vmem((NX, 2, 64, 512), BF16),
            vmem((NX, 2, 64, 512), BF16),
            vmem((2 * NYL, PIECE, 512), F32),
            vmem((2 * NYL, PIECE, 512), BF16),
            vmem((2 * NYL, PIECE, 512), BF16),
            vmem((NZ, PIECE, 512), BF16),
            vmem((NYL, PIECE, 512), F32),
        ]
        + [dma((HALF,))] * 12
        + [
            dma((2,)), dma((NX,)), dma((NX,)), dma((2 * NYL,)), dma((2 * NYL,)),
            dma((NZ,)), dma((NZ,)), dma((NYL,)), dma((NYL,)),
        ],
        compiler_params=pltpu.CompilerParams(collective_id=0, has_side_effects=True),
    )(query, key, value, gate_u, out_grad, lengths, norm_gain.reshape(1, 512), out_weight)


def solution(mesh):
    split = P(("grp", "blk"), None)
    return jax.shard_map(
        shards,
        mesh=mesh,
        in_specs=(split,) * 5 + (P("grp"), P(), P()),
        out_specs=(split,) * 5 + (P(None, "blk"),),
        check_vma=False,
    )
```

time: 213 us -> 89.6 us (0.42)
  the two profiles are of different devices: /device:TPU:8 before, /device:TPU:1 now
where the time goes in v2:
time: 89.6 us; the launch traced here: 89.4 us
  Pallas kernels  81.8 us (91%)
  local copies, waits for them, and re-layouts  6.27 us (7%)
  between operations  1.3 us (1%)
    pallas_call x1, Pallas kernels, shards(): pl.pallas_call(layer_kernel, out_shape=(jax.ShapeDtypeStruct((rows, 1024)...  81.8 us
    unnamed x15, local copies, waits for them, and re-layouts  4.51 us

profile of v2, /device:TPU:1, one launch (start us, length us, event | category | flops | bytes accessed | tf_op | source)
XLA Modules:
  0.0 89.4 jit_solution(3709720625741822334)
XLA Ops:
  1.3 81.8 %shard_map.127 = (bf16[128,1024]{1,0:T(8,128)(2,1)}, bf16[128,512]{1,0:T(8,128)(2,1)}, bf16[128,512]{1,0:T(8,128)(2,1)}, bf16[128,512]{1,0:T(8,128)(2,1)}, bf16[128,512]{1,0:T(8,128)(2,1)}, /*index=5*/f32[512,64]{1,0:T(8,128)}) custom-call(bf16[128,512]{1,0:T(8,128)(2,1)} %q_ref.1, bf16[128,512]{1,0:T(8,128)(2,1)} %k_ref.1, bf16[128,512]{1,0:T(8,128)(2,1)} %v_ref.1, ...), custom_call_target="tpu_custom_call" | custom-call | tf_op jit(solution)/shard_map/pallas_call | solution.py:429
  83.1 0.0 copy-start
  83.1 1.8 %copy.14 = f32[512,64]{0,1:T(8,128)} copy(f32[512,64]{1,0:T(8,128)} %get-tuple-element.11) | data formatting | bytes 262144 | tf_op jit(solution)/shard_map/pallas_call | solution.py:429
  84.9 0.0 copy-done
  84.9 0.0 copy-start.4
  84.9 0.7 copy.21
  85.6 0.3 copy-done.4
  85.9 0.0 copy-start.3
  85.9 0.7 copy.22
  86.5 0.3 copy-done.3
  86.8 0.0 copy-start.2
  86.8 0.7 copy.23
  87.5 0.3 copy-done.2
  87.8 0.0 copy-start.1
  87.8 0.7 copy.24
  88.4 0.3 copy-done.1
  88.7 0.7 copy.25
Async XLA Ops:
  83.1 1.8 %copy-start = (bf16[128,1024]{1,0:T(8,128)(2,1)S(1)}, bf16[128,1024]{1,0:T(8,128)(2,1)}, u32[]{:S(2)}) copy-start(bf16[128,1024]{1,0:T(8,128)(2,1)} %get-tuple-element.18) | copy-start | bytes 786436
  84.9 1.0 %copy-start.4 = (bf16[128,512]{1,0:T(8,128)(2,1)S(1)}, bf16[128,512]{1,0:T(8,128)(2,1)}, u32[]{:S(2)}) copy-start(bf16[128,512]{1,0:T(8,128)(2,1)} %get-tuple-element.19) | copy-start | bytes 393220
  85.9 1.0 %copy-start.3 = (bf16[128,512]{1,0:T(8,128)(2,1)S(1)}, bf16[128,512]{1,0:T(8,128)(2,1)}, u32[]{:S(2)}) copy-start(bf16[128,512]{1,0:T(8,128)(2,1)} %get-tuple-element.20) | copy-start | bytes 393220
  86.8 1.0 %copy-start.2 = (bf16[128,512]{1,0:T(8,128)(2,1)S(1)}, bf16[128,512]{1,0:T(8,128)(2,1)}, u32[]{:S(2)}) copy-start(bf16[128,512]{1,0:T(8,128)(2,1)} %get-tuple-element.21) | copy-start | bytes 393220
  87.8 1.0 %copy-start.1 = (bf16[128,512]{1,0:T(8,128)(2,1)S(1)}, bf16[128,512]{1,0:T(8,128)(2,1)}, u32[]{:S(2)}) copy-start(bf16[128,512]{1,0:T(8,128)(2,1)} %get-tuple-element.22) | copy-start | bytes 393220

commit v3 on v2

v3 whole, which is shorter than its diff:
```python
import jax
import jax.numpy as jnp
from jax import lax
from jax.experimental import pallas as pl
from jax.experimental.pallas import tpu as pltpu
from jax.sharding import PartitionSpec as P

MESH = pl.DeviceIdType.MESH
EPS = 1e-05
ZA = 4
ZB = 3
NZ = ZA * ZB
NYL = 4
NX = 4
HALF = 8
ROWS = 128
TILE = 512
F32 = jnp.float32
BF16 = jnp.bfloat16


def where_am_i():
    g, b = (lax.axis_index("grp"), lax.axis_index("blk"))
    return (g // NZ, g % NZ, b // 8, (b // 2) % NX, b % 2)


def device(y_lo, z, y_hi, x, core):
    return (y_lo * NZ + z, (y_hi * NX + x) * 2 + core)


def remote(src, dst, send_sem, recv_sem, target):
    return pltpu.make_async_remote_copy(
        src_ref=src, dst_ref=dst, send_sem=send_sem, recv_sem=recv_sem,
        device_id=target, device_id_type=MESH,
    )


def swap(part):
    return pltpu.roll(part.astype(F32), 64, 1)


def low_lanes(rows):
    return lax.broadcasted_iota(jnp.int32, (rows, 128), 1) < 64


def fold_rows(block, odd):
    low = low_lanes(64)
    top, bottom = (block[:64], block[64:])
    if odd:
        return jnp.where(low, swap(top), bottom.astype(F32))
    return jnp.where(low, top.astype(F32), swap(bottom))


def join_heads(even, odd):
    low = low_lanes(even.shape[0])
    return (jnp.where(low, even, swap(odd)), jnp.where(low, swap(even), odd))


def nt(left, right):
    return lax.dot_general(left, right, (((1,), (1,)), ((), ())), preferred_element_type=F32)


def tn(left, right):
    return lax.dot_general(left, right, (((0,), (0,)), ((), ())), preferred_element_type=F32)


def nn(left, right):
    return jnp.dot(left, right, preferred_element_type=F32)


def symmetric_partners(me):
    y_lo, z, y_hi, x, core = me
    mine = (y_hi * NX + x) * 2 + core
    y = y_hi * NYL + y_lo
    found = [(y_lo * NZ + z, (mine + d) % 16) for d in range(1, 16)]
    for d in range(1, 2 * NYL):
        if d != NYL:
            to = (y + d) % (2 * NYL)
            found.append(device(to % NYL, z, to // NYL, x, core))
    for d in range(1, ZA):
        found.append(device(y_lo, near_z(z, d), y_hi, x, core))
    for d in range(1, ZB):
        found.append(device(y_lo, far_z(z, d), y_hi, x, core))
    for d in range(1, NYL):
        for cc in range(2):
            found.append(device((y_lo + d) % NYL, z, y_hi, y_lo, cc))
    return found


def near_z(z, d):
    return z // ZA * ZA + (z % ZA + d) % ZA


def far_z(z, d):
    return (z // ZA + d) % ZB * ZA + z % ZA


def layer_kernel(
    q_hbm, k_hbm, v_hbm, gate_hbm, cot_hbm, length_hbm, gain_hbm, weight_hbm,
    out_ref, gq_ref, gk_ref, gv_ref, gg_ref, gw_ref,
    q_ref, k_ref, v_ref, gate_ref, length_ref, gain_ref, weight_ref,
    in_send, in_got, side_send, side_got, up_got, cot_all, gain_cols,
    qf, dot_ref, att_acc, stat_send, stat_got, mix_send, mix_got,
    dkv_acc, dqt_acc, up_acc, back_send, back_got, down_send, down_got,
    y_own, y_send, y_got, near_all, far_all, fin_send, fin_got, fin_turned,
    load, in_ss, in_rs, side_ss, side_rs, up_ss, up_rs, cot_ss, cot_rs, rel_ss, rel_rs,
    stat_ss, stat_rs, mix_ss, mix_rs, back_ss, back_rs, down_ss, down_rs,
    y_ss, y_rs, near_ss, near_rs, far_ss, far_rs, fin_ss, fin_rs,
):
    me = where_am_i()
    y_lo, z, y_hi, x, core = me
    g = y_lo * NZ + z
    y = y_hi * NYL + y_lo
    h = x * 2 + core
    base = y_hi * HALF
    upper = y_hi == 1
    lower = y_hi == 0

    loads = [
        pltpu.make_async_copy(k_hbm, k_ref, load.at[0]),
        pltpu.make_async_copy(v_hbm, v_ref, load.at[1]),
        pltpu.make_async_copy(q_hbm, q_ref, load.at[2]),
        pltpu.make_async_copy(gate_hbm, gate_ref, load.at[3]),
        pltpu.make_async_copy(cot_hbm, cot_all.at[h], load.at[4]),
        pltpu.make_async_copy(weight_hbm, weight_ref, load.at[5]),
        pltpu.make_async_copy(gain_hbm, gain_ref, load.at[6]),
        pltpu.make_async_copy(length_hbm, length_ref, load.at[7]),
    ]
    for copy in loads:
        copy.start()

    def far_sources():
        return [device(x, z, y_hi, xx, cc) for xx in range(NX) for cc in range(2)]

    barrier = pltpu.get_barrier_semaphore()
    partners = symmetric_partners(me)
    for target in partners:
        pl.semaphore_signal(barrier, inc=1, device_id=target, device_id_type=MESH)

    @pl.when(x != y_lo)
    def _():
        for target in far_sources():
            pl.semaphore_signal(barrier, inc=1, device_id=target, device_id_type=MESH)

    for copy in loads[:3]:
        copy.wait()
    low128 = low_lanes(128)
    for t in range(HALF):
        cols = slice((t // 2) * 128, (t // 2 + 1) * 128)
        kk, vv = (k_ref[:, cols], v_ref[:, cols])
        if t % 2:
            pair = jnp.where(low128, swap(kk), vv.astype(F32))
        else:
            pair = jnp.where(low128, kk.astype(F32), swap(vv))
        in_send[t, 64:192] = pair.astype(BF16)
        in_send[t, 0:64] = (fold_rows(q_ref[:, cols], t % 2) * 0.0625).astype(BF16)
    in_got[h] = in_send[h]

    @pl.when(x != y_lo)
    def _():
        pl.semaphore_wait(barrier, len(partners) + HALF)

    @pl.when(x == y_lo)
    def _():
        pl.semaphore_wait(barrier, len(partners))

    def up_copy(t):
        return remote(
            in_send.at[t, pl.ds(64, 128)], up_got.at[h], up_ss.at[t], up_rs.at[h], (g, HALF + t)
        )

    def up_arrival(s):
        return remote(
            in_send.at[s, pl.ds(64, 128)], up_got.at[s], up_ss.at[s], up_rs.at[s], (g, s)
        )

    @pl.when(lower)
    def _():
        for t in range(HALF):
            up_copy(t).start()

    def to_half(send, got, ssem, rsem):
        copies = []
        for d in range(1, HALF):
            t = (h + d) % HALF
            copies.append(remote(send.at[t], got.at[h], ssem.at[d], rsem.at[d], (g, base + t)))
        for copy in copies:
            copy.start()
        return copies

    def from_half(send, got, ssem, rsem):
        for d in range(1, HALF):
            t = (h + d) % HALF
            s = (h + HALF - d) % HALF
            remote(send.at[t], got.at[s], ssem.at[d], rsem.at[d], (g, base + t)).wait_recv()

    sent = to_half(in_send, in_got, in_ss, in_rs)

    for copy in loads[3:7]:
        copy.wait()
    for p in range(HALF // 2):
        cols = slice(p * 128, (p + 1) * 128)
        turned = gate_ref[:, cols].astype(F32).T.astype(BF16)
        side_send[2 * p, 0:64] = turned[:64]
        side_send[2 * p + 1, 0:64] = turned[64:]
        spread = jnp.broadcast_to(gain_ref[:, cols], (128, 128)).T
        gain_cols[2 * p] = spread[:64]
        gain_cols[2 * p + 1] = spread[64:]
        grads = nt(weight_ref[cols], cot_all[h]).astype(BF16)
        side_send[2 * p, 64:128] = grads[:64]
        side_send[2 * p + 1, 64:128] = grads[64:]
    side_got[h] = side_send[h]
    sent += to_half(side_send, side_got, side_ss, side_rs)

    sister = (g, base + h + 1 - 2 * core)
    for d in range(1, NX):
        copy = remote(
            cot_all.at[h], cot_all.at[h], cot_ss.at[d], cot_rs.at[d],
            device(y_lo, z, y_hi, (x + d) % NX, core),
        )
        copy.start()
        sent.append(copy)

    def relay(d):
        slot = (x + NX - d) % NX * 2 + core
        return remote(cot_all.at[slot], cot_all.at[slot], rel_ss.at[d], rel_rs.at[d], sister)

    def relay_arrival(d):
        slot = (x + NX - d) % NX * 2 + 1 - core
        return remote(cot_all.at[slot], cot_all.at[slot], rel_ss.at[d], rel_rs.at[d], sister)

    first = relay(0)
    first.start()
    sent.append(first)

    from_half(in_send, in_got, in_ss, in_rs)
    low64 = low_lanes(64)
    for s in range(HALF):
        folded = in_got[s, 0:64].astype(F32)
        qf[s * 128:s * 128 + 64] = jnp.where(low64, folded, 0.0).astype(BF16)
        qf[s * 128 + 64:s * 128 + 128] = jnp.where(low64, swap(folded), 0.0).astype(BF16)
    att_acc[...] = jnp.zeros_like(att_acc)
    dkv_acc[...] = jnp.zeros_like(dkv_acc)
    dqt_acc[...] = jnp.zeros_like(dqt_acc)

    def local_kv(j):
        return in_got[pl.ds(j * 4, 4), 64:192].reshape(TILE, 128)

    def upper_kv(j):
        return up_got[pl.ds(j * 4, 4)].reshape(TILE, 128)

    def rows_of(i):
        return pl.ds(pl.multiple_of(i * TILE, TILE), TILE)

    tile_row = lax.broadcasted_iota(jnp.int32, (TILE, TILE), 0)
    tile_col = lax.broadcasted_iota(jnp.int32, (TILE, TILE), 1)

    def forward_tile(i, kv, diagonal):
        half_score = nt(kv, qf[rows_of(i)])
        weight = half_score + half_score * jnp.tanh(half_score)
        if diagonal:
            weight = jnp.where(tile_row <= tile_col, weight, 0.0)
        att_acc[i] += tn(kv[:, 64:], weight.astype(BF16))

    @pl.loop(0, 2)
    def _(i):
        forward_tile(i, local_kv(i), True)

    forward_tile(1, local_kv(0), False)
    from_half(side_send, side_got, side_ss, side_rs)
    loads[7].wait()
    gates = jnp.concatenate([side_got[s, 0:64] for s in range(HALF)], axis=1).astype(F32)
    grads = jnp.concatenate([side_got[s, 64:128] for s in range(HALF)], axis=1).astype(F32)
    gain = gain_cols[h][:, 0:1]
    normed_grad = grads * gates * gain
    position = base * ROWS + lax.broadcasted_iota(jnp.int32, (1, HALF * ROWS), 1)
    alive = position < length_ref[0]

    @pl.when(upper)
    def _():
        for j in range(2):
            for s in range(4):
                up_arrival(4 * j + s).wait_recv()

            @pl.loop(0, 2)
            def _(i):
                forward_tile(i, upper_kv(j), False)

    attended = jnp.where(alive, jnp.concatenate([att_acc[0], att_acc[1]], axis=1), 0.0)
    mean_mine = jnp.sum(attended, axis=0, keepdims=True) * (1.0 / 64)
    centre = attended - mean_mine
    stats = (
        mean_mine,
        jnp.sum(centre * centre, axis=0, keepdims=True),
        jnp.sum(normed_grad, axis=0, keepdims=True),
        jnp.sum(normed_grad * centre, axis=0, keepdims=True),
    )
    for n, stat in enumerate(stats):
        stat_send[n:n + 1] = stat[:, :TILE]
        stat_send[n + 4:n + 5] = stat[:, TILE:]
    stat_got[h] = stat_send[...]
    for d in range(1, HALF):
        t = (h + d) % HALF
        copy = remote(stat_send, stat_got.at[h], stat_ss.at[d], stat_rs.at[d], (g, base + t))
        copy.start()
        sent.append(copy)
    for d in range(1, NX):
        slot = (x + NX - d) % NX * 2 + core
        remote(
            cot_all.at[h], cot_all.at[slot], cot_ss.at[d], cot_rs.at[d],
            device(y_lo, z, y_hi, (x + d) % NX, core),
        ).wait_recv()
        copy = relay(d)
        copy.start()
        sent.append(copy)
    for d in range(1, HALF):
        t = (h + d) % HALF
        s = (h + HALF - d) % HALF
        remote(
            stat_send, stat_got.at[s], stat_ss.at[d], stat_rs.at[d], (g, base + t)
        ).wait_recv()

    def stat_rows(n):
        return [
            jnp.concatenate([stat_got[s, n:n + 1], stat_got[s, n + 4:n + 5]], axis=1)
            for s in range(HALF)
        ]

    means, squares, sums, products = (stat_rows(n) for n in range(4))
    mean = sum(means) * (1.0 / HALF)
    square = sum(squares)
    grad_sum = sum(sums)
    product = sum(products)
    for s in range(HALF):
        off = means[s] - mean
        square = square + 64.0 * (off * off)
        product = product + off * sums[s]
    inv_std = lax.rsqrt(square * (1.0 / 512) + EPS)
    grad_mean = grad_sum * (1.0 / 512)
    product_mean = inv_std * product * (1.0 / 512)
    normed = (attended - mean) * inv_std
    scaled = normed * gain
    mixed = (scaled * gates).astype(BF16)
    grad_gate = (grads * scaled).astype(BF16)
    attended_grad = inv_std * (normed_grad - grad_mean - normed * product_mean)
    attended_grad = jnp.where(alive, attended_grad, 0.0).astype(BF16)
    dot_ref[0:64] = jnp.zeros_like(attended_grad)
    dot_ref[64:128] = attended_grad
    for s in range(HALF):
        mix_send[s, 0:64] = mixed[:, s * 128:(s + 1) * 128]
        mix_send[s, 64:128] = grad_gate[:, s * 128:(s + 1) * 128]
    mix_got[h] = mix_send[h]
    sent += to_half(mix_send, mix_got, mix_ss, mix_rs)

    for d in range(NX):
        relay_arrival(d).wait_recv()
    for n in range(2 * NYL):
        part = nn(mixed, cot_all[:, :, n * 128:(n + 1) * 128].reshape(HALF * ROWS, 128))
        y_own[n] = part
        y_send[n] = part.astype(BF16)
    to_y = []
    for d in range(1, 2 * NYL):
        to = (y + d) % (2 * NYL)
        copy = remote(
            y_send.at[to], y_got.at[d], y_ss.at[d], y_rs.at[d],
            device(to % NYL, z, to // NYL, x, core),
        )
        copy.start()
        to_y.append(copy)

    def columns_of(i):
        return pl.ds(pl.multiple_of(i * TILE, TILE), TILE)

    def backward_tile(i, kv, diagonal):
        qs, dots = (qf[rows_of(i)], dot_ref[:, columns_of(i)])
        half_score = nt(kv, qs)
        grad = nn(kv, dots)
        tanh = jnp.tanh(half_score)
        plus = 1.0 + tanh
        weight = half_score * plus
        slope = grad * (plus + weight * (1.0 - tanh))
        if diagonal:
            keep = tile_row <= tile_col
            weight = jnp.where(keep, weight, 0.0)
            slope = jnp.where(keep, slope, 0.0)
        slope = slope.astype(BF16)
        dqt_acc[i] += tn(kv[:, :64], slope)
        return nn(slope, qs) + nt(weight.astype(BF16), dots)

    def down_copy(s):
        return remote(down_send.at[s], down_got.at[h], down_ss.at[s], down_rs.at[h], (g, s))

    def down_arrival(t):
        return remote(
            down_send.at[t], down_got.at[t], down_ss.at[t], down_rs.at[t], (g, HALF + t)
        )

    @pl.when(upper)
    def _():
        for j in range(2):
            up_acc[...] = jnp.zeros_like(up_acc)

            @pl.loop(0, 2)
            def _(i):
                up_acc[...] += backward_tile(i, upper_kv(j), False)

            for s in range(4):
                down_send[4 * j + s] = up_acc[s * 128:(s + 1) * 128].astype(BF16)
                down_copy(4 * j + s).start()

    total = y_own[y]
    for d in range(1, 2 * NYL):
        to_y[d - 1].wait_recv()
        total = total + y_got[d].astype(F32)
    near_all[z % ZA] = total.astype(BF16)
    for d in range(1, ZA):
        copy = remote(
            near_all.at[z % ZA], near_all.at[z % ZA], near_ss.at[d], near_rs.at[d],
            device(y_lo, near_z(z, d), y_hi, x, core),
        )
        copy.start()
        sent.append(copy)

    @pl.loop(0, 2)
    def _(i):
        dkv_acc[rows_of(i)] += backward_tile(i, local_kv(i), True)

    dkv_acc[0:TILE] += backward_tile(1, local_kv(0), False)

    for s in range(HALF):
        i, at = (s // 4, (s % 4) * 128)
        back_send[s, 0:64] = (dqt_acc[i, :, at:at + 128] * 0.0625).astype(BF16)
        back_send[s, 64:192] = dkv_acc[s * 128:(s + 1) * 128].astype(BF16)
    back_got[h] = back_send[h]
    sent += to_half(back_send, back_got, back_ss, back_rs)

    for d in range(1, ZA):
        remote(
            near_all.at[z % ZA], near_all.at[(z % ZA + ZA - d) % ZA], near_ss.at[d], near_rs.at[d],
            device(y_lo, near_z(z, d), y_hi, x, core),
        ).wait_recv()
    total = near_all[0].astype(F32)
    for n in range(1, ZA):
        total = total + near_all[n].astype(F32)
    far_all[z // ZA] = total.astype(BF16)
    for d in range(1, ZB):
        copy = remote(
            far_all.at[z // ZA], far_all.at[z // ZA], far_ss.at[d], far_rs.at[d],
            device(y_lo, far_z(z, d), y_hi, x, core),
        )
        copy.start()
        sent.append(copy)

    from_half(mix_send, mix_got, mix_ss, mix_rs)
    whole = jnp.concatenate([mix_got[t, 0:64] for t in range(HALF)], axis=0)
    out_ref[...] = tn(whole, weight_ref[...]).astype(BF16)
    for p in range(HALF // 2):
        pair = jnp.concatenate(
            [mix_got[2 * p, 64:128].astype(F32), mix_got[2 * p + 1, 64:128].astype(F32)], axis=0
        )
        gg_ref[:, p * 128:(p + 1) * 128] = pair.T.astype(BF16)

    for d in range(1, ZB):
        remote(
            far_all.at[z // ZA], far_all.at[(z // ZA + ZB - d) % ZB], far_ss.at[d], far_rs.at[d],
            device(y_lo, far_z(z, d), y_hi, x, core),
        ).wait_recv()
    total = far_all[0].astype(F32)
    for n in range(1, ZB):
        total = total + far_all[n].astype(F32)
    fin_send[...] = total.astype(BF16)

    def fin_copy(lo, cc):
        return remote(
            fin_send, fin_got.at[h], fin_ss.at[lo * 2 + cc], fin_rs.at[h],
            device(lo, z, y_hi, y_lo, cc),
        )

    def not_me(lo, cc):
        return (x != y_lo) | (lo != y_lo) | (cc != core)

    for lo in range(NYL):
        for cc in range(2):

            @pl.when(not_me(lo, cc))
            def _():
                fin_copy(lo, cc).start()

    @pl.when(x == y_lo)
    def _():
        fin_got[h] = fin_send[...]

    from_half(back_send, back_got, back_ss, back_rs)
    for p in range(HALF // 2):
        pair = jnp.concatenate(
            [back_got[2 * p, 0:64].astype(F32), back_got[2 * p + 1, 0:64].astype(F32)], axis=0
        )
        gq_ref[:, p * 128:(p + 1) * 128] = pair.T.astype(BF16)

    @pl.when(lower)
    def _():
        for t in range(HALF):
            down_arrival(t).wait_recv()

    for p in range(HALF // 2):
        cols = slice(p * 128, (p + 1) * 128)
        heads = []
        for t in (2 * p, 2 * p + 1):
            mine = back_got[t, 64:192].astype(F32)
            far = jnp.where(lower, down_got[t].astype(F32), 0.0)
            heads.append(mine + far)
        kk, vv = join_heads(*heads)
        gk_ref[:, cols] = kk.astype(BF16)
        gv_ref[:, cols] = vv.astype(BF16)

    for xx in range(NX):
        for cc in range(2):
            t = xx * 2 + cc

            @pl.when((x != y_lo) | (h != t))
            def _():
                remote(
                    fin_send, fin_got.at[t], fin_ss.at[t], fin_rs.at[t],
                    device(x, z, y_hi, xx, cc),
                ).wait_recv()

    for p in range(HALF // 2):
        pair = jnp.concatenate(
            [fin_got[2 * p].astype(F32), fin_got[2 * p + 1].astype(F32)], axis=0
        )
        fin_turned[:, p * 128:(p + 1) * 128] = pair.T
    gw_ref[...] = fin_turned[pl.ds(pl.multiple_of(core * 64, 64), 64)]

    for copy in sent + to_y:
        copy.wait_send()
    for lo in range(NYL):
        for cc in range(2):

            @pl.when(not_me(lo, cc))
            def _():
                fin_copy(lo, cc).wait_send()

    @pl.when(lower)
    def _():
        for t in range(HALF):
            up_copy(t).wait_send()

    @pl.when(upper)
    def _():
        for s in range(HALF):
            down_copy(s).wait_send()


def shards(query, key, value, gate_u, out_grad, lengths, norm_gain, out_weight):
    dma = pltpu.SemaphoreType.DMA
    vmem = pltpu.VMEM
    rows = query.shape[0]
    outs = [((rows, 1024), BF16)] + [((rows, 512), BF16)] * 4 + [((64, 512), F32)]
    results = pl.pallas_call(
        layer_kernel,
        out_shape=tuple(vmem(*out) for out in outs),
        in_specs=[pl.BlockSpec(memory_space=pl.ANY)] * 8,
        out_specs=(pl.BlockSpec(memory_space=vmem),) * 6,
        scratch_shapes=[
            vmem((ROWS, 512), BF16),
            vmem((ROWS, 512), BF16),
            vmem((ROWS, 512), BF16),
            vmem((ROWS, 512), BF16),
            pltpu.SMEM((1,), jnp.int32),
            vmem((1, 512), F32),
            vmem((512, 1024), BF16),
            vmem((HALF, 192, 128), BF16),
            vmem((HALF, 192, 128), BF16),
            vmem((HALF, 128, 128), BF16),
            vmem((HALF, 128, 128), BF16),
            vmem((HALF, 128, 128), BF16),
            vmem((HALF, ROWS, 1024), BF16),
            vmem((HALF, 64, 128), F32),
            vmem((1024, 128), BF16),
            vmem((128, 1024), BF16),
            vmem((2, 64, TILE), F32),
            vmem((8, TILE), F32),
            vmem((HALF, 8, TILE), F32),
            vmem((HALF, 128, 128), BF16),
            vmem((HALF, 128, 128), BF16),
            vmem((1024, 128), F32),
            vmem((2, 64, TILE), F32),
            vmem((TILE, 128), F32),
            vmem((HALF, 192, 128), BF16),
            vmem((HALF, 192, 128), BF16),
            vmem((HALF, 128, 128), BF16),
            vmem((HALF, 128, 128), BF16),
            vmem((2 * NYL, 64, 128), F32),
            vmem((2 * NYL, 64, 128), BF16),
            vmem((2 * NYL, 64, 128), BF16),
            vmem((ZA, 64, 128), BF16),
            vmem((ZB, 64, 128), BF16),
            vmem((64, 128), BF16),
            vmem((HALF, 64, 128), BF16),
            vmem((128, 512), F32),
        ]
        + [dma((HALF,))] * 27,
        compiler_params=pltpu.CompilerParams(collective_id=0, has_side_effects=True),
    )(query, key, value, gate_u, out_grad, lengths, norm_gain.reshape(1, 512), out_weight)
    anywhere = pl.BlockSpec(memory_space=pl.ANY)
    results = pl.pallas_call(
        store_kernel,
        out_shape=tuple(jax.ShapeDtypeStruct(*out) for out in outs),
        in_specs=[pl.BlockSpec(memory_space=vmem)] * 6,
        out_specs=(anywhere,) * 6,
        scratch_shapes=[dma((6,))],
    )(*[pltpu.with_memory_space_constraint(one, vmem) for one in results])
    return (*results[:5], results[5].T)


def store_kernel(*refs):
    sources, targets, sems = (refs[:6], refs[6:12], refs[12])
    copies = [
        pltpu.make_async_copy(source, target, sems.at[n])
        for n, (source, target) in enumerate(zip(sources, targets))
    ]
    for copy in copies:
        copy.start()
    for copy in copies:
        copy.wait()


def solution(mesh):
    split = P(("grp", "blk"), None)
    return jax.shard_map(
        shards,
        mesh=mesh,
        in_specs=(split,) * 5 + (P("grp"), P(), P()),
        out_specs=(split,) * 5 + (P(None, "blk"),),
        check_vma=False,
    )
```

time: 89.6 us -> 79.8 us (0.89)
  the two profiles are of different devices: /device:TPU:1 before, /device:TPU:5 now
where the time goes in v3:
time: 79.8 us; the launch traced here: 79.7 us
  Pallas kernels  78.4 us (98%)
  between operations  1.29 us (2%)
    pallas_call x1, Pallas kernels, shards(): pl.pallas_call(layer_kernel, out_shape=tuple((vmem(*out) for out in outs)...  77.4 us

profile of v3, /device:TPU:5, one launch (start us, length us, event | category | flops | bytes accessed | tf_op | source)
XLA Modules:
  0.0 79.7 jit_solution(196386764661550520)
XLA Ops:
  1.3 77.4 %shard_map.127 = (bf16[128,1024]{1,0:T(8,128)(2,1)S(1)}, bf16[128,512]{1,0:T(8,128)(2,1)S(1)}, bf16[128,512]{1,0:T(8,128)(2,1)S(1)}, bf16[128,512]{1,0:T(8,128)(...) custom-call(bf16[128,512]{1,0:T(8,128)(2,1)} %q_hbm.1, bf16[128,512]{1,0:T(8,128)(2,1)} %k_hbm.1, ...), custom_call_target="tpu_custom_call" | custom-call | tf_op jit(solution)/shard_map/pallas_call | solution.py:559
  78.7 1.0 %shard_map.128 = (bf16[128,1024]{1,0:T(8,128)(2,1)}, bf16[128,512]{1,0:T(8,128)(2,1)}, bf16[128,512]{1,0:T(8,128)(2,1)}, bf16[128,512]{1,0:T(8,128)(2,1)}, bf16[128,512]{1,0:T(8,128)(2,1)}, /*index=5*/f32[64,512]{1,0:T(8,128)}) custom-call(bf16[128,1024]{1,0:T(8,128)(2,1)S(1)} %get-tuple-element.18.refs_0_, bf16[128,512]{1,0:T(8,128)(2,1)S(1)} %get-tuple-element.19.refs_1_, ...), custom_call_target="tpu_custom_call" | custom-call | tf_op jit(solution)/shard_map/pallas_call | solution.py:606

commit v4 on v3

--- a/solution.py
+++ b/solution.py
@@ -213,11 +213,17 @@
     sent += to_half(side_send, side_got, side_ss, side_rs)
 
     sister = (g, base + h + 1 - 2 * core)
-    for d in range(1, NX):
-        copy = remote(
-            cot_all.at[h], cot_all.at[h], cot_ss.at[d], cot_rs.at[d],
-            device(y_lo, z, y_hi, (x + d) % NX, core),
-        )
+
+    def slot_of(d):
+        return (x + NX - d) % NX * 2 + core
+
+    def to_chip(part, d, n):
+        return remote(
+            part, part, cot_ss.at[n], cot_rs.at[n], device(y_lo, z, y_hi, (x + d) % NX, core)
+        )
+
+    for d in (1, 3):
+        copy = to_chip(cot_all.at[h], d, d)
         copy.start()
         sent.append(copy)
 
@@ -267,6 +273,16 @@
         forward_tile(i, local_kv(i), True)
 
     forward_tile(1, local_kv(0), False)
+    to_chip(cot_all.at[slot_of(1)], 1, 1).wait_recv()
+    to_chip(cot_all.at[slot_of(3)], 3, 3).wait_recv()
+    for copy in (
+        to_chip(cot_all.at[slot_of(1), pl.ds(0, 64)], 1, 4),
+        to_chip(cot_all.at[slot_of(3), pl.ds(64, 64)], 3, 5),
+        relay(1),
+        relay(3),
+    ):
+        copy.start()
+        sent.append(copy)
     from_half(side_send, side_got, side_ss, side_rs)
     loads[7].wait()
     gates = jnp.concatenate([side_got[s, 0:64] for s in range(HALF)], axis=1).astype(F32)
@@ -304,15 +320,11 @@
         copy = remote(stat_send, stat_got.at[h], stat_ss.at[d], stat_rs.at[d], (g, base + t))
         copy.start()
         sent.append(copy)
-    for d in range(1, NX):
-        slot = (x + NX - d) % NX * 2 + core
-        remote(
-            cot_all.at[h], cot_all.at[slot], cot_ss.at[d], cot_rs.at[d],
-            device(y_lo, z, y_hi, (x + d) % NX, core),
-        ).wait_recv()
-        copy = relay(d)
-        copy.start()
-        sent.append(copy)
+    to_chip(cot_all.at[slot_of(2), pl.ds(0, 64)], 1, 4).wait_recv()
+    to_chip(cot_all.at[slot_of(2), pl.ds(64, 64)], 3, 5).wait_recv()
+    copy = relay(2)
+    copy.start()
+    sent.append(copy)
     for d in range(1, HALF):
         t = (h + d) % HALF
         s = (h + HALF - d) % HALF
@@ -408,6 +420,19 @@
                 down_send[4 * j + s] = up_acc[s * 128:(s + 1) * 128].astype(BF16)
                 down_copy(4 * j + s).start()
 
+    @pl.loop(0, 2)
+    def _(i):
+        dkv_acc[rows_of(i)] += backward_tile(i, local_kv(i), True)
+
+    dkv_acc[0:TILE] += backward_tile(1, local_kv(0), False)
+
+    for s in range(HALF):
+        i, at = (s // 4, (s % 4) * 128)
+        back_send[s, 0:64] = (dqt_acc[i, :, at:at + 128] * 0.0625).astype(BF16)
+        back_send[s, 64:192] = dkv_acc[s * 128:(s + 1) * 128].astype(BF16)
+    back_got[h] = back_send[h]
+    sent += to_half(back_send, back_got, back_ss, back_rs)
+
     total = y_own[y]
     for d in range(1, 2 * NYL):
         to_y[d - 1].wait_recv()
@@ -421,18 +446,14 @@
         copy.start()
         sent.append(copy)
 
-    @pl.loop(0, 2)
-    def _(i):
-        dkv_acc[rows_of(i)] += backward_tile(i, local_kv(i), True)
-
-    dkv_acc[0:TILE] += backward_tile(1, local_kv(0), False)
-
-    for s in range(HALF):
-        i, at = (s // 4, (s % 4) * 128)
-        back_send[s, 0:64] = (dqt_acc[i, :, at:at + 128] * 0.0625).astype(BF16)
-        back_send[s, 64:192] = dkv_acc[s * 128:(s + 1) * 128].astype(BF16)
-    back_got[h] = back_send[h]
-    sent += to_half(back_send, back_got, back_ss, back_rs)
+    from_half(mix_send, mix_got, mix_ss, mix_rs)
+    whole = jnp.concatenate([mix_got[t, 0:64] for t in range(HALF)], axis=0)
+    out_ref[...] = tn(whole, weight_ref[...]).astype(BF16)
+    for p in range(HALF // 2):
+        pair = jnp.concatenate(
+            [mix_got[2 * p, 64:128].astype(F32), mix_got[2 * p + 1, 64:128].astype(F32)], axis=0
+        )
+        gg_ref[:, p * 128:(p + 1) * 128] = pair.T.astype(BF16)
 
     for d in range(1, ZA):
         remote(
@@ -451,14 +472,12 @@
         copy.start()
         sent.append(copy)
 
-    from_half(mix_send, mix_got, mix_ss, mix_rs)
-    whole = jnp.concatenate([mix_got[t, 0:64] for t in range(HALF)], axis=0)
-    out_ref[...] = tn(whole, weight_ref[...]).astype(BF16)
+    from_half(back_send, back_got, back_ss, back_rs)
     for p in range(HALF // 2):
         pair = jnp.concatenate(
-            [mix_got[2 * p, 64:128].astype(F32), mix_got[2 * p + 1, 64:128].astype(F32)], axis=0
-        )
-        gg_ref[:, p * 128:(p + 1) * 128] = pair.T.astype(BF16)
+            [back_got[2 * p, 0:64].astype(F32), back_got[2 * p + 1, 0:64].astype(F32)], axis=0
+        )
+        gq_ref[:, p * 128:(p + 1) * 128] = pair.T.astype(BF16)
 
     for d in range(1, ZB):
         remote(
@@ -489,13 +508,6 @@
     @pl.when(x == y_lo)
     def _():
         fin_got[h] = fin_send[...]
-
-    from_half(back_send, back_got, back_ss, back_rs)
-    for p in range(HALF // 2):
-        pair = jnp.concatenate(
-            [back_got[2 * p, 0:64].astype(F32), back_got[2 * p + 1, 0:64].astype(F32)], axis=0
-        )
-        gq_ref[:, p * 128:(p + 1) * 128] = pair.T.astype(BF16)
 
     @pl.when(lower)
     def _():

time: 79.8 us -> 78.7 us (0.986)
  Pallas kernels: 78.4 us -> 77.2 us
    pallas_call x1, Pallas kernels: 77.4 us -> 76.3 us  [shards(): pl.pallas_call(layer_kernel, out_shape=tuple((vmem(*out) for out in outs)...]
where the time goes in v4:
time: 78.7 us; the launch traced here: 78.5 us
  Pallas kernels  77.2 us (98%)
  between operations  1.29 us (2%)
    pallas_call x1, Pallas kernels, shards(): pl.pallas_call(layer_kernel, out_shape=tuple((vmem(*out) for out in outs)...  76.3 us

profile of v4, /device:TPU:5, one launch (start us, length us, event | category | flops | bytes accessed | tf_op | source)
XLA Modules:
  0.0 78.5 jit_solution(5699309651480342164)
XLA Ops:
  1.3 76.3 %shard_map.127 = (bf16[128,1024]{1,0:T(8,128)(2,1)S(1)}, bf16[128,512]{1,0:T(8,128)(2,1)S(1)}, bf16[128,512]{1,0:T(8,128)(2,1)S(1)}, bf16[128,512]{1,0:T(8,128)(...) custom-call(bf16[128,512]{1,0:T(8,128)(2,1)} %q_hbm.1, bf16[128,512]{1,0:T(8,128)(2,1)} %k_hbm.1, ...), custom_call_target="tpu_custom_call" | custom-call | tf_op jit(solution)/shard_map/pallas_call | solution.py:571
  77.6 1.0 %shard_map.128 = (bf16[128,1024]{1,0:T(8,128)(2,1)}, bf16[128,512]{1,0:T(8,128)(2,1)}, bf16[128,512]{1,0:T(8,128)(2,1)}, bf16[128,512]{1,0:T(8,128)(2,1)}, bf16[128,512]{1,0:T(8,128)(2,1)}, /*index=5*/f32[64,512]{1,0:T(8,128)}) custom-call(bf16[128,1024]{1,0:T(8,128)(2,1)S(1)} %get-tuple-element.18.refs_0_, bf16[128,512]{1,0:T(8,128)(2,1)S(1)} %get-tuple-element.19.refs_1_, ...), custom_call_target="tpu_custom_call" | custom-call | tf_op jit(solution)/shard_map/pallas_call | solution.py:618

commit v5 on v4

--- a/solution.py
+++ b/solution.py
@@ -174,9 +174,12 @@
             in_send.at[s, pl.ds(64, 128)], up_got.at[s], up_ss.at[s], up_rs.at[s], (g, s)
         )
 
+    def heads_at(d):
+        return [(x + d) % NX * 2 + cc for cc in range(2)]
+
     @pl.when(lower)
     def _():
-        for t in range(HALF):
+        for t in heads_at(0):
             up_copy(t).start()
 
     def to_half(send, got, ssem, rsem):
@@ -195,6 +198,12 @@
             remote(send.at[t], got.at[s], ssem.at[d], rsem.at[d], (g, base + t)).wait_recv()
 
     sent = to_half(in_send, in_got, in_ss, in_rs)
+
+    @pl.when(lower)
+    def _():
+        for d in (1, 3, 2):
+            for t in heads_at(d):
+                up_copy(t).start()
 
     for copy in loads[3:7]:
         copy.wait()
@@ -418,7 +427,6 @@
 
             for s in range(4):
                 down_send[4 * j + s] = up_acc[s * 128:(s + 1) * 128].astype(BF16)
-                down_copy(4 * j + s).start()
 
     @pl.loop(0, 2)
     def _(i):
@@ -432,6 +440,12 @@
         back_send[s, 64:192] = dkv_acc[s * 128:(s + 1) * 128].astype(BF16)
     back_got[h] = back_send[h]
     sent += to_half(back_send, back_got, back_ss, back_rs)
+
+    @pl.when(upper)
+    def _():
+        for d in (0, 1, 3, 2):
+            for s in heads_at(d):
+                down_copy(s).start()
 
     total = y_own[y]
     for d in range(1, 2 * NYL):
@@ -472,13 +486,6 @@
         copy.start()
         sent.append(copy)
 
-    from_half(back_send, back_got, back_ss, back_rs)
-    for p in range(HALF // 2):
-        pair = jnp.concatenate(
-            [back_got[2 * p, 0:64].astype(F32), back_got[2 * p + 1, 0:64].astype(F32)], axis=0
-        )
-        gq_ref[:, p * 128:(p + 1) * 128] = pair.T.astype(BF16)
-
     for d in range(1, ZB):
         remote(
             far_all.at[z // ZA], far_all.at[(z // ZA + ZB - d) % ZB], far_ss.at[d], far_rs.at[d],
@@ -508,6 +515,13 @@
     @pl.when(x == y_lo)
     def _():
         fin_got[h] = fin_send[...]
+
+    from_half(back_send, back_got, back_ss, back_rs)
+    for p in range(HALF // 2):
+        pair = jnp.concatenate(
+            [back_got[2 * p, 0:64].astype(F32), back_got[2 * p + 1, 0:64].astype(F32)], axis=0
+        )
+        gq_ref[:, p * 128:(p + 1) * 128] = pair.T.astype(BF16)
 
     @pl.when(lower)
     def _():

time: 78.7 us -> 71.1 us (0.903)
  Pallas kernels: 77.2 us -> 69.6 us
    pallas_call x1, Pallas kernels: 76.3 us -> 68.7 us  [shards(): pl.pallas_call(layer_kernel, out_shape=tuple((vmem(*out) for out in outs)...]
where the time goes in v5:
time: 71.1 us; the launch traced here: 70.9 us
  Pallas kernels  69.6 us (98%)
  between operations  1.29 us (2%)
    pallas_call x1, Pallas kernels, shards(): pl.pallas_call(layer_kernel, out_shape=tuple((vmem(*out) for out in outs)...  68.7 us

profile of v5, /device:TPU:5, one launch (start us, length us, event | category | flops | bytes accessed | tf_op | source)
XLA Modules:
  0.0 70.9 jit_solution(5227933689928921237)
XLA Ops:
  1.3 68.7 %shard_map.127 = (bf16[128,1024]{1,0:T(8,128)(2,1)S(1)}, bf16[128,512]{1,0:T(8,128)(2,1)S(1)}, bf16[128,512]{1,0:T(8,128)(2,1)S(1)}, bf16[128,512]{1,0:T(8,128)(...) custom-call(bf16[128,512]{1,0:T(8,128)(2,1)} %q_hbm.1, bf16[128,512]{1,0:T(8,128)(2,1)} %k_hbm.1, ...), custom_call_target="tpu_custom_call" | custom-call | tf_op jit(solution)/shard_map/pallas_call | solution.py:585
  70.0 1.0 %shard_map.128 = (bf16[128,1024]{1,0:T(8,128)(2,1)}, bf16[128,512]{1,0:T(8,128)(2,1)}, bf16[128,512]{1,0:T(8,128)(2,1)}, bf16[128,512]{1,0:T(8,128)(2,1)}, bf16[128,512]{1,0:T(8,128)(2,1)}, /*index=5*/f32[64,512]{1,0:T(8,128)}) custom-call(bf16[128,1024]{1,0:T(8,128)(2,1)S(1)} %get-tuple-element.18.refs_0_, bf16[128,512]{1,0:T(8,128)(2,1)S(1)} %get-tuple-element.19.refs_1_, ...), custom_call_target="tpu_custom_call" | custom-call | tf_op jit(solution)/shard_map/pallas_call | solution.py:632
